TPU v7x, 8 devices: a whole 2x2x1 slice. The times are simulated.
8 devices in a mesh: dp: 2 (over z, y), ep: 4 (over x, core).
Axes of the slice: x: 2, y: 2, z: 1, core: 2. Of those that a mesh axis runs over, the one named last changes fastest.
Arguments:
- w_gate: bfloat16 [1, 8, 4096, 1536], P(None, 'ep')
- w_up: bfloat16 [1, 8, 4096, 1536], P(None, 'ep')
- w_down: bfloat16 [1, 8, 1536, 4096], P(None, 'ep')
- place: int32 [1, 32], replicated
Outputs:
- output 1: bfloat16 [1, 32, 4096, 3072], P(None, ('dp', 'ep'))
- output 2: bfloat16 [1, 32, 1536, 4096], P(None, ('dp', 'ep'))
All inputs are finite; a program needn't handle non-finite values.
Results may differ from a plain program's by a relative error of at most 0.001.
Values are sent between devices in bfloat16 or wider.
A program may use at most 1 GiB of HBM per device.

v0:
```python
import functools

import jax
import jax.numpy as jnp
from jax import lax
from jax.experimental import pallas as pl
from jax.experimental.pallas import tpu as pltpu
from jax.sharding import PartitionSpec as P


TILE = 512
NBUF = 4
VMEM_LIMIT = 40 * 1024 * 1024
BOTH_ROWS = 768
LAST_ROWS = (640, 112, 16)


def _shard(dp, ep, slots, a, g, j):
    return (2 * a - g) % ep if j < ((a + 1) * slots) // dp else (g + j + 1) % ep


def _devices(dp, ep, slots, flip):
    return [[a * ep + g for a in range(dp) for g in range(ep) if _shard(dp, ep, slots, a, g, j) == g ^ flip]
            for j in range(slots)]


def _any(me, devices):
    hit = me < 0
    for n in sorted(set(devices)):
        hit = jnp.logical_or(hit, me == n)
    return hit


def _tiles(rows, tile):
    out, r = [], 0
    for n in [tile // 8, tile // 4, tile - tile // 8 - tile // 4] + [tile] * rows:
        n = min(n, rows - r)
        if n:
            out.append((r, n))
        r += n
    return out


def _stream(steps, read, writes):
    for t in range(min(NBUF, steps)):
        read(t).start()
    for t in range(steps):
        read(t).wait()
        writes(t, lambda c: c.start())
        writes(t, lambda c: c.wait())
        if t + NBUF < steps:
            read(t + NBUF).start()


def _both(src, dests, experts, who, me, buf, rsem, wsem):
    tiles = _tiles(src.shape[1], buf.shape[2])

    def read(t):
        r, n = tiles[t]
        return pltpu.make_async_copy(src.at[:, pl.ds(r, n)], buf.at[t % NBUF, :, pl.ds(0, n)], rsem.at[t % NBUF])

    def writes(t, act):
        r, n = tiles[t]
        for j, dest in enumerate(dests):
            if who[j]:
                @pl.when(_any(me, who[j]))
                def _():
                    act(pltpu.make_async_copy(buf.at[t % NBUF, experts[j], pl.ds(0, n)], dest(r, n),
                                              wsem.at[t % NBUF, j]))

    _stream(len(tiles), read, writes)


def _one(src, dests, wanted, buf, rsem, wsem):
    tiles = _tiles(src.shape[0], buf.shape[2])

    def read(t):
        r, n = tiles[t]
        return pltpu.make_async_copy(src.at[pl.ds(r, n)], buf.at[t % NBUF, 0, pl.ds(0, n)], rsem.at[t % NBUF])

    def writes(t, act):
        r, n = tiles[t]
        for j, dest in enumerate(dests):
            def go():
                act(pltpu.make_async_copy(buf.at[t % NBUF, 0, pl.ds(0, n)], dest(r, n), wsem.at[t % NBUF, j]))

            if wanted[j] is True:
                go()
            elif wanted[j] is not None:
                pl.when(wanted[j])(go)

    _stream(len(tiles), read, writes)


def solution(mesh):
    dp = mesh.shape["dp"]
    ep = mesh.shape["ep"]
    axes = ("dp", "ep")
    hbm = pl.BlockSpec(memory_space=pltpu.HBM)
    vmem = pl.BlockSpec(memory_space=pltpu.VMEM)
    smem = pl.BlockSpec(memory_space=pltpu.SMEM)

    def hand_over(w_gate, w_up, w_down, place):
        wg, wu, wd = w_gate[0], w_up[0], w_down[0]
        n_exp, D, F = wg.shape
        slots = place.shape[1] // (dp * ep)
        own, across, beside, relayed = (_devices(dp, ep, slots, f) for f in (0, 2, 1, 3))
        to_x = [(n ^ 2, n) for n in sorted(set(sum(across, [])) | {m ^ 1 for m in sum(relayed, [])})]
        to_core = [(n ^ 1, n) for n in sorted(set(sum(beside, [])))]
        to_relay = [(n ^ 1, n) for n in sorted(set(sum(relayed, [])))]

        def ring(cols, tile, experts=n_exp):
            return [pltpu.VMEM((NBUF, experts, tile, cols), jnp.bfloat16),
                    pltpu.SemaphoreType.DMA((NBUF,)), pltpu.SemaphoreType.DMA((NBUF, slots))]

        def where():
            return lax.axis_index("dp") * ep + lax.axis_index("ep")

        def half(out, j, k):
            return lambda r, n: out.at[j, pl.ds(r, n), pl.ds(k * F, F)]

        def rows_of(out, j, first):
            return lambda r, n: out.at[j, pl.ds(first + r, n)]

        def picks(place_ref, me):
            return [lax.rem(place_ref[0, me * slots + j], n_exp) for j in range(slots)]

        def early(pick, me, flip):
            e = me * 0
            for _, n in to_x:
                on = [j for j in range(slots) if n ^ 1 in relayed[j]]
                here = [j for j in range(slots) if n in across[j]]
                if on:
                    first = pick(n ^ 1, on[0])
                else:
                    first = jnp.where(2 * sum(pick(n, j) for j in here) > len(here), 1, 0)
                e = jnp.where(me == n ^ flip, first, e)
            return e

        def scalars(place_ref):
            return lambda n, j: lax.rem(place_ref[0, n * slots + j], n_exp)

        def bits(place_ref):
            lane = lax.broadcasted_iota(jnp.int32, place_ref.shape, 1)
            mask = jnp.sum(jnp.left_shift(jnp.bitwise_and(place_ref[...], 1), lane))
            return lambda n, j: jnp.bitwise_and(jnp.right_shift(mask, n * slots + j), 1)

        def call(kernel, out_shape, in_specs, scratch, size, aliases=None):
            return pl.pallas_call(
                kernel, out_shape=out_shape, in_specs=in_specs,
                out_specs=jax.tree.map(lambda _: hbm, out_shape), scratch_shapes=scratch,
                input_output_aliases=aliases or {},
                compiler_params=pltpu.CompilerParams(vmem_limit_bytes=VMEM_LIMIT),
                cost_estimate=pl.CostEstimate(flops=0, bytes_accessed=size, transcendentals=0))

        def own_kernel(place_ref, g, u, d, cg, cu, cd, o13, o2, buf_f, rf, wf, buf_d, rd, wd_):
            me = where()
            e = picks(place_ref, me)

            many = [n for n in range(dp * ep) if sum(n in d for d in own) > 1]

            @pl.when(_any(me, many))
            def _():
                _both(g, [half(o13, j, 0) for j in range(slots)], e, own, me, buf_f, rf, wf)
                _both(u, [half(o13, j, 1) for j in range(slots)], e, own, me, buf_f, rf, wf)
                _both(d, [rows_of(o2, j, 0) for j in range(slots)], e, own, me, buf_d, rd, wd_)

            for who, blocks in ((own, (g, u, d)), (beside, (cg, cu, cd))):
                for j in range(slots):
                    single = [n for n in who[j] if who is beside or n not in many]
                    if single:
                        @pl.when(_any(me, single))
                        def _():
                            _one(blocks[0].at[e[j]], [half(o13, j, 0)], [True], buf_f, rf, wf)
                            _one(blocks[1].at[e[j]], [half(o13, j, 1)], [True], buf_f, rf, wf)
                            _one(blocks[2].at[e[j]], [rows_of(o2, j, 0)], [True], buf_d, rd, wd_)

        def both_kernel(dest, place_ref, got, rel, _, out, buf, rs, ws):
            me = where()
            e = picks(place_ref, me)

            @pl.when(_any(me, sum(across, [])))
            def _():
                _both(got, [dest(out, j) for j in range(slots)], e, across, me, buf, rs, ws)

            for j in range(slots):
                if relayed[j]:
                    @pl.when(_any(me, relayed[j]))
                    def _():
                        _one(rel.at[e[j]], [dest(out, j)], [True], buf, rs, ws)

        def wants(pick, me, first):
            a = early(pick, me, 0)
            return [jnp.logical_and(_any(me, across[j]), (pick(me, j) == a) == first) if across[j] else None
                    for j in range(slots)]

        def first_kernel(dest, place_ref, got, rel, _, out, buf, rs, ws):
            me = where()

            @pl.when(_any(me, sum(across, [])))
            def _():
                _one(got, [dest(out, j) for j in range(slots)], wants(scalars(place_ref), me, True), buf, rs, ws)

            for j in range(slots):
                if relayed[j]:
                    @pl.when(_any(me, relayed[j]))
                    def _():
                        copy = pltpu.make_async_copy(rel, dest(out, j)(0, rel.shape[0]), rs.at[0])
                        copy.start()
                        copy.wait()

        def other_kernel(dest, place_ref, got, _, out, buf, rs, ws):
            me = where()

            @pl.when(_any(me, sum(across, [])))
            def _():
                _one(got, [dest(out, j) for j in range(slots)], wants(scalars(place_ref), me, False), buf, rs, ws)

        def last_kernel(dest, place_ref, got, _, out, ws):
            want = wants(bits(place_ref), where(), False)
            for act in (lambda c: c.start(), lambda c: c.wait()):
                for j in range(slots):
                    if want[j] is not None:
                        @pl.when(want[j])
                        def _():
                            act(pltpu.make_async_copy(got, dest(out, j)(0, got.shape[0]), ws.at[j]))

        def cut_kernel(place_ref, d, both, *rest):
            pieces, (buf, rs, ws) = rest[:-3], rest[-3:]
            e = early(scalars(place_ref), where(), 2)
            tile = buf.shape[2]
            steps = [(d.at[x, pl.ds(r, n)], both.at[x, pl.ds(r, n)], n)
                     for x in range(n_exp) for r, n in _tiles(BOTH_ROWS, tile)]
            first = BOTH_ROWS
            for i, o in enumerate(pieces):
                x = e if i == 0 else 1 - e
                for r, n in _tiles(o.shape[0], tile):
                    steps.append((d.at[x, pl.ds(first + r, n)], o.at[pl.ds(r, n)], n))
                first = BOTH_ROWS if i == 0 else first + o.shape[0]

            def read(t):
                src, _, n = steps[t]
                return pltpu.make_async_copy(src, buf.at[t % NBUF, 0, pl.ds(0, n)], rs.at[t % NBUF])

            def writes(t, act):
                _, dst, n = steps[t]
                act(pltpu.make_async_copy(buf.at[t % NBUF, 0, pl.ds(0, n)], dst, ws.at[t % NBUF, 0]))

            _stream(len(steps), read, writes)

        def permute(x, pairs):
            return lax.ppermute(x, axes, pairs)

        def shape(*dims):
            return jax.ShapeDtypeStruct(dims, jnp.bfloat16)

        block = wg.size * wg.dtype.itemsize
        got_g = permute(wg, to_x)
        got_u = permute(wu, to_x)
        cuts = call(cut_kernel,
                    [shape(n_exp, BOTH_ROWS, D), shape(F - BOTH_ROWS, D)] + [shape(n, D) for n in LAST_ROWS],
                    [smem, hbm], ring(D, TILE // 2, 1), 2 * block)(place, wd)
        got_d = [permute(c, to_x) for c in cuts]
        side = [permute(w, to_core) for w in (wg, wu, wd)]
        w13, w2 = call(own_kernel, (shape(slots, D, 2 * F), shape(slots, F, D)),
                       [smem] + [hbm] * 6, ring(F, TILE) + ring(D, TILE // 4), 6 * block)(place, wg, wu, wd, *side)

        def later(kernel, dest, got, out, cols, tile, rel_in=hbm):
            rel = permute(got, to_relay)
            return call(functools.partial(kernel, dest), shape(*out.shape), [smem, hbm, rel_in, hbm],
                        ring(cols, tile), 3 * got.size * 2, {3: 0})(place, got, rel, out)

        w13 = later(both_kernel, lambda o, j: half(o, j, 0), got_g, w13, F, TILE)
        w13 = later(both_kernel, lambda o, j: half(o, j, 1), got_u, w13, F, TILE)
        w2 = later(both_kernel, lambda o, j: rows_of(o, j, 0), got_d[0], w2, D, TILE // 4)
        w2 = later(first_kernel, lambda o, j: rows_of(o, j, BOTH_ROWS), got_d[1], w2, D, TILE // 2,
                   vmem)
        r = BOTH_ROWS
        for i, got in enumerate(got_d[2:]):
            kernel, ins, scratch = ((other_kernel, [smem, hbm, hbm], ring(D, TILE // 4, 1)) if i == 0 else
                                    (last_kernel, [vmem, vmem, hbm], [pltpu.SemaphoreType.DMA((slots,))]))
            w2 = call(functools.partial(kernel, lambda o, j, r=r: rows_of(o, j, r)),
                      shape(*w2.shape), ins, scratch, 3 * got.size * 2, {2: 0})(place, got, w2)
            r += got.shape[0]
        return w13[None], w2[None]

    spec_in = P(None, "ep", None, None)
    spec_out = P(None, ("dp", "ep"), None, None)
    return jax.shard_map(hand_over, mesh=mesh,
                         in_specs=(spec_in, spec_in, spec_in, P(None, None)),
                         out_specs=(spec_out, spec_out), check_vma=False)
```

profile of v0, /device:TPU:3, one launch (start us, length us, event | category | flops | bytes accessed | tf_op | source)
XLA Modules:
  0.0 1004.6 jit_solution(14347636849961563261)
XLA Ops:
  0.6 1.9 collective-permute-start.2
  2.6 3.4 collective-permute-start
  6.6 21.8 %shard_map.62 = (bf16[2,768,4096]{2,1,0:T(8,128)(2,1)}, bf16[768,4096]{1,0:T(8,128)(2,1)S(1)}, bf16[640,4096]{1,0:T(8,128)(2,1)}, bf16[112,4096]{1,0:T(8,128)(2,1)}, bf16[16,4096]{1,0:T(8,128)(2,1)S(1)}) custom-call(s32[1,32]{1,0:T(1,128)S(1)} %copy-done.3, bf16[2,1536,4096]{2,1,0:T(8,128)(2,1)} %bitcast.8), custom_call_target="tpu_custom_call" | custom-call | bytes 50331648 | tf_op jit(solution)/shard_map/pallas_call | solution.py:260
  29.0 1.9 collective-permute-start.12
  30.9 3.4 collective-permute-start.10
  35.6 711.1 %collective-permute-done.10.got = bf16[768,4096]{1,0:T(8,128)(2,1)S(1)} collective-permute-done((bf16[768,4096]{1,0:T(8,128)(2,1)S(1)}, bf16[768,4096]{1,0:T(8,128)(2,1)S(1)}, u32[]{:S(2)}, u32[]{:S(2)}) %collective-permute-start.10) | collective-permute-done | bytes 6291488 | tf_op jit(solution)/shard_map/ppermute | solution.py:252
  749.7 8.1 collective-permute-done.11.rel
  757.7 2.7 copy-done.1
  761.7 19.6 %collective-permute-start.3 = (bf16[2,4096,1536]{2,1,0:T(8,128)(2,1)}, bf16[2,4096,1536]{2,1,0:T(8,128)(2,1)}, u32[]{:S(2)}, u32[]{:S(2)}) collective-permute-start(bf16[2,4096,1536]{2,1,0:T(8,128)(2,1)} %collective-permute-done.2.got), channel_id=1, source_target_pairs={{1,0},{3,2}} | collective-permute-start | bytes 75497480 | tf_op jit(solution)/shard_map/ppermute | solution.py:252
  781.3 9.5 collective-permute-start.1
  790.8 5.9 collective-permute-start.13
  796.7 4.5 copy-done
  801.1 8.3 copy-done.5
  809.4 1.9 collective-permute-start.9
  811.3 12.4 %collective-permute-done.6.cd = bf16[2,1536,4096]{2,1,0:T(8,128)(2,1)} collective-permute-done((bf16[2,1536,4096]{2,1,0:T(8,128)(2,1)}, bf16[2,1536,4096]{2,1,0:T(8,128)(2,1)}, u32[]{:S(2)}, u32[]{:S(2)}) %collective-permute-start.6) | collective-permute-done | bytes 25165856 | tf_op jit(solution)/shard_map/ppermute | solution.py:252
  823.8 1.9 collective-permute-start.8
  825.7 38.3 %collective-permute-done.13.rel = bf16[2,768,4096]{2,1,0:T(8,128)(2,1)} collective-permute-done((bf16[2,768,4096]{2,1,0:T(8,128)(2,1)S(1)}, bf16[2,768,4096]{2,1,0:T(8,128)(2,1)}, u32[]{:S(2)}, u32[]{:S(2)}) %collective-permute-start.13) | collective-permute-done | bytes 12582944 | tf_op jit(solution)/shard_map/ppermute | solution.py:252
  864.0 2.3 collective-permute-start.7
  866.4 74.4 %shard_map.59 = (bf16[4,4096,3072]{2,1,0:T(8,128)(2,1)}, bf16[4,1536,4096]{2,1,0:T(8,128)(2,1)}) custom-call(s32[1,32]{1,0:T(1,128)S(1)} %copy-done.3, bf16[2,4096,1536]{2,1,0:T(8,128)(2,1)} %bitcast.16, bf16[2,4096,1536]{2,1,0:T(8,128)(2,1)} %bitcast.13, bf16[2,1536,4096]{2,1,0:T(8,128)(2,1)} %bitcast.10, bf16[2,4096,1536]{2,1,0:T(8,128)(2,1)} %collective-permute-done.4.cg, ...), custom_call_target="tpu_custom_call" | custom-call | bytes 150994944 | tf_op jit(solution)/shard_map/pallas_call | solution.py:265
  940.8 10.7 %shard_map.63._ = bf16[4,1536,4096]{2,1,0:T(8,128)(2,1)} custom-call(s32[1,32]{1,0:T(1,128)S(1)} %copy-done.3, bf16[2,768,4096]{2,1,0:T(8,128)(2,1)S(1)} %bitcast.6, bf16[2,768,4096]{2,1,0:T(8,128)(2,1)} %collective-permute-done.13.rel, bf16[4,1536,4096]{2,1,0:T(8,128)(2,1)} %get-tuple-element.15._), custom_call_target="tpu_custom_call", output_to_operand_aliasing={{}: (3, {})} | custom-call | bytes 37748736 | tf_op jit(solution)/shard_map/pallas_call | solution.py:270
  951.5 2.8 copy-done.2
  955.5 9.2 shard_map.65._
  968.0 18.3 %shard_map.60._ = bf16[4,4096,3072]{2,1,0:T(8,128)(2,1)} custom-call(s32[1,32]{1,0:T(1,128)S(1)} %copy-done.3, bf16[2,4096,1536]{2,1,0:T(8,128)(2,1)} %collective-permute-done.2.got, bf16[2,4096,1536]{2,1,0:T(8,128)(2,1)} %collective-permute-done.3.rel, bf16[4,4096,3072]{2,1,0:T(8,128)(2,1)} %get-tuple-element.9._), custom_call_target="tpu_custom_call", output_to_operand_aliasing={{}: (3, {})} | custom-call | bytes 75497472 | tf_op jit(solution)/shard_map/pallas_call | solution.py:270
  986.3 18.3 %shard_map.61 = bf16[4,4096,3072]{2,1,0:T(8,128)(2,1)} custom-call(s32[1,32]{1,0:T(1,128)S(1)} %copy-done.3, bf16[2,4096,1536]{2,1,0:T(8,128)(2,1)} %collective-permute-done.got, bf16[2,4096,1536]{2,1,0:T(8,128)(2,1)} %collective-permute-done.1.rel, bf16[4,4096,3072]{2,1,0:T(8,128)(2,1)} %shard_map.60._), custom_call_target="tpu_custom_call", output_to_operand_aliasing={{}: (3, {})} | custom-call | bytes 75497472 | tf_op jit(solution)/shard_map/pallas_call | solution.py:270
  (32 shorter events, 11.3 us)
Async XLA Ops:
  0.6 761.1 %collective-permute-start.2 = (bf16[2,4096,1536]{2,1,0:T(8,128)(2,1)}, bf16[2,4096,1536]{2,1,0:T(8,128)(2,1)}, u32[]{:S(2)}, u32[]{:S(2)}) collective-permute-start(bf16[2,4096,1536]{2,1,0:T(8,128)(2,1)} %bitcast.14), channel_id=1, source_target_pairs={{3,1},{1,3},{6,4},{4,6}} | collective-permute-start | bytes 75497480 | tf_op jit(solution)/shard_map/ppermute | solution.py:252
  2.6 778.7 %collective-permute-start = (bf16[2,4096,1536]{2,1,0:T(8,128)(2,1)}, bf16[2,4096,1536]{2,1,0:T(8,128)(2,1)}, u32[]{:S(2)}, u32[]{:S(2)}) collective-permute-start(bf16[2,4096,1536]{2,1,0:T(8,128)(2,1)} %bitcast.11), channel_id=1, source_target_pairs={{3,1},{1,3},{6,4},{4,6}} | collective-permute-start | bytes 75497480 | tf_op jit(solution)/shard_map/ppermute | solution.py:252
  5.9 0.7 copy-start.3
  28.4 0.6 copy-start.4
  29.0 719.4 %collective-permute-start.12 = (bf16[2,768,4096]{2,1,0:T(8,128)(2,1)}, bf16[2,768,4096]{2,1,0:T(8,128)(2,1)S(1)}, u32[]{:S(2)}, u32[]{:S(2)}) collective-permute-start(bf16[2,768,4096]{2,1,0:T(8,128)(2,1)} %get-tuple-element.14), channel_id=1, source_target_pairs={{3,1},{1,3},{6,4},{4,6}} | collective-permute-start | bytes 37748744 | tf_op jit(solution)/shard_map/ppermute | solution.py:252
  30.9 715.7 %collective-permute-start.10 = (bf16[768,4096]{1,0:T(8,128)(2,1)S(1)}, bf16[768,4096]{1,0:T(8,128)(2,1)S(1)}, u32[]{:S(2)}, u32[]{:S(2)}) collective-permute-start(bf16[768,4096]{1,0:T(8,128)(2,1)S(1)} %get-tuple-element.13), channel_id=1, source_target_pairs={{3,1},{1,3},{6,4},{4,6}} | collective-permute-start | bytes 18874376 | tf_op jit(solution)/shard_map/ppermute | solution.py:252
  34.3 756.5 %collective-permute-start.4 = (bf16[2,4096,1536]{2,1,0:T(8,128)(2,1)}, bf16[2,4096,1536]{2,1,0:T(8,128)(2,1)}, u32[]{:S(2)}, u32[]{:S(2)}) collective-permute-start(bf16[2,4096,1536]{2,1,0:T(8,128)(2,1)} %bitcast.15), channel_id=1, source_target_pairs={{0,1},{2,3}} | collective-permute-start | bytes 75497480 | tf_op jit(solution)/shard_map/ppermute | solution.py:252
  746.7 11.1 %collective-permute-start.11 = (bf16[768,4096]{1,0:T(8,128)(2,1)S(1)}, bf16[768,4096]{1,0:T(8,128)(2,1)S(1)}, u32[]{:S(2)}, u32[]{:S(2)}) collective-permute-start(bf16[768,4096]{1,0:T(8,128)(2,1)S(1)} %collective-permute-done.10.got), channel_id=1, source_target_pairs={{1,0},{3,2}} | collective-permute-start | bytes 18874376 | tf_op jit(solution)/shard_map/ppermute | solution.py:252
  748.4 52.7 %collective-permute-start.5 = (bf16[2,4096,1536]{2,1,0:T(8,128)(2,1)}, bf16[2,4096,1536]{2,1,0:T(8,128)(2,1)S(1)}, u32[]{:S(2)}, u32[]{:S(2)}) collective-permute-start(bf16[2,4096,1536]{2,1,0:T(8,128)(2,1)} %bitcast.12), channel_id=1, source_target_pairs={{0,1},{2,3}} | collective-permute-start | bytes 75497480 | tf_op jit(solution)/shard_map/ppermute | solution.py:252
  757.7 2.7 copy-start.1
  760.4 63.4 %collective-permute-start.6 = (bf16[2,1536,4096]{2,1,0:T(8,128)(2,1)}, bf16[2,1536,4096]{2,1,0:T(8,128)(2,1)}, u32[]{:S(2)}, u32[]{:S(2)}) collective-permute-start(bf16[2,1536,4096]{2,1,0:T(8,128)(2,1)} %bitcast.9), channel_id=1, source_target_pairs={{0,1},{2,3}} | collective-permute-start | bytes 75497480 | tf_op jit(solution)/shard_map/ppermute | solution.py:252
  761.7 206.3 %collective-permute-start.3 = (bf16[2,4096,1536]{2,1,0:T(8,128)(2,1)}, bf16[2,4096,1536]{2,1,0:T(8,128)(2,1)}, u32[]{:S(2)}, u32[]{:S(2)}) collective-permute-start(bf16[2,4096,1536]{2,1,0:T(8,128)(2,1)} %collective-permute-done.2.got), channel_id=1, source_target_pairs={{1,0},{3,2}} | collective-permute-start | bytes 75497480 | tf_op jit(solution)/shard_map/ppermute | solution.py:252
  781.3 205.0 %collective-permute-start.1 = (bf16[2,4096,1536]{2,1,0:T(8,128)(2,1)}, bf16[2,4096,1536]{2,1,0:T(8,128)(2,1)}, u32[]{:S(2)}, u32[]{:S(2)}) collective-permute-start(bf16[2,4096,1536]{2,1,0:T(8,128)(2,1)} %collective-permute-done.got), channel_id=1, source_target_pairs={{1,0},{3,2}} | collective-permute-start | bytes 75497480 | tf_op jit(solution)/shard_map/ppermute | solution.py:252
  790.8 73.2 %collective-permute-start.13 = (bf16[2,768,4096]{2,1,0:T(8,128)(2,1)S(1)}, bf16[2,768,4096]{2,1,0:T(8,128)(2,1)}, u32[]{:S(2)}, u32[]{:S(2)}) collective-permute-start(bf16[2,768,4096]{2,1,0:T(8,128)(2,1)S(1)} %collective-permute-done.12.got), channel_id=1, source_target_pairs={{1,0},{3,2}} | collective-permute-start | bytes 37748744 | tf_op jit(solution)/shard_map/ppermute | solution.py:252
  796.7 4.5 copy-start
  801.1 8.3 copy-start.5
  809.4 146.1 %collective-permute-start.9 = (bf16[640,4096]{1,0:T(8,128)(2,1)}, bf16[640,4096]{1,0:T(8,128)(2,1)S(1)}, u32[]{:S(2)}, u32[]{:S(2)}) collective-permute-start(bf16[640,4096]{1,0:T(8,128)(2,1)} %get-tuple-element.12), channel_id=1, source_target_pairs={{3,1},{1,3},{6,4},{4,6}} | collective-permute-start | bytes 15728648 | tf_op jit(solution)/shard_map/ppermute | solution.py:252
  823.8 141.0 %collective-permute-start.8 = (bf16[112,4096]{1,0:T(8,128)(2,1)}, bf16[112,4096]{1,0:T(8,128)(2,1)S(1)}, u32[]{:S(2)}, u32[]{:S(2)}) collective-permute-start(bf16[112,4096]{1,0:T(8,128)(2,1)} %get-tuple-element.11), channel_id=1, source_target_pairs={{3,1},{1,3},{6,4},{4,6}} | collective-permute-start | bytes 2752520 | tf_op jit(solution)/shard_map/ppermute | solution.py:252
  864.0 76.7 %slice-start = ((s8[12582912]{0:T(1024)(128)(4,1)}), s8[4194304]{0:T(1024)(128)(4,1)S(1)}, s32[]{:S(2)}) async-start(s8[12582912]{0:T(1024)(128)(4,1)} %bitcast.5), calls=%async_computation | async-start | bytes 8388608
  864.0 76.7 %slice-start.1 = ((s8[12582912]{0:T(1024)(128)(4,1)}), s8[4194304]{0:T(1024)(128)(4,1)S(1)}, s32[]{:S(2)}) async-start(s8[12582912]{0:T(1024)(128)(4,1)} %bitcast.5), calls=%async_computation.1 | async-start | bytes 8388608
  864.0 76.7 %slice-start.2 = ((s8[12582912]{0:T(1024)(128)(4,1)}), s8[4194304]{0:T(1024)(128)(4,1)S(1)}, s32[]{:S(2)}) async-start(s8[12582912]{0:T(1024)(128)(4,1)} %bitcast.5), calls=%async_computation.2 | async-start | bytes 8388608
  864.0 102.1 %collective-permute-start.7 = (bf16[16,4096]{1,0:T(8,128)(2,1)}, bf16[16,4096]{1,0:T(8,128)(2,1)}, u32[]{:S(2)}, u32[]{:S(2)}) collective-permute-start(bf16[16,4096]{1,0:T(8,128)(2,1)} %copy-done.4), channel_id=1, source_target_pairs={{3,1},{1,3},{6,4},{4,6}} | collective-permute-start | bytes 393224 | tf_op jit(solution)/shard_map/ppermute | solution.py:252
  951.5 2.8 copy-start.2
where the time goes:
time: 1010 us; the launch traced here: 1000 us
  waiting for transfers between devices  770 us (76%)
  Pallas kernels  157 us (16%)
  starting transfers between devices  57.2 us (6%)
  local copies, waits for them, and re-layouts  19.5 us (2%)
    ppermute x14, waiting for transfers between devices, permute(): return lax.ppermute(x, axes, pairs)  770 us
    pallas_call x1, Pallas kernels, hand_over(): call(own_kernel, (shape(slots, D, 2 * F), shape(slots, F, D)), [smem] + [...  74.4 us
    ppermute x14, starting transfers between devices, permute(): return lax.ppermute(x, axes, pairs)  57.2 us
    pallas_call x4, Pallas kernels, later(): call(functools.partial(kernel, dest), shape(*out.shape), [smem, hbm, rel_...  48.5 us
    pallas_call x1, Pallas kernels, hand_over(): call(cut_kernel, [shape(n_exp, BOTH_ROWS, D), shape(F - BOTH_ROWS, D)] +...  21.8 us
  transfers between devices with their start and end apart: 14, of which 4 were waited for; matrix products, arithmetic and copies ran while one was open for 0% of the time, Pallas kernels for 14%

commit v1 on v0

--- a/solution.py
+++ b/solution.py
@@ -10,9 +10,10 @@
 
 TILE = 512
 NBUF = 4
-VMEM_LIMIT = 40 * 1024 * 1024
+VMEM_LIMIT = 36 * 1024 * 1024
+VMEM_LIMIT_WIDE = 44 * 1024 * 1024
 BOTH_ROWS = 768
-LAST_ROWS = (640, 112, 16)
+LAST_ROWS = (656, 96, 16)
 
 
 def _shard(dp, ep, slots, a, g, j):
@@ -145,12 +146,12 @@
             mask = jnp.sum(jnp.left_shift(jnp.bitwise_and(place_ref[...], 1), lane))
             return lambda n, j: jnp.bitwise_and(jnp.right_shift(mask, n * slots + j), 1)
 
-        def call(kernel, out_shape, in_specs, scratch, size, aliases=None):
+        def call(kernel, out_shape, in_specs, scratch, size, aliases=None, cols=0):
             return pl.pallas_call(
                 kernel, out_shape=out_shape, in_specs=in_specs,
                 out_specs=jax.tree.map(lambda _: hbm, out_shape), scratch_shapes=scratch,
                 input_output_aliases=aliases or {},
-                compiler_params=pltpu.CompilerParams(vmem_limit_bytes=VMEM_LIMIT),
+                compiler_params=pltpu.CompilerParams(vmem_limit_bytes=VMEM_LIMIT_WIDE if cols == F else VMEM_LIMIT),
                 cost_estimate=pl.CostEstimate(flops=0, bytes_accessed=size, transcendentals=0))
 
         def own_kernel(place_ref, g, u, d, cg, cu, cd, o13, o2, buf_f, rf, wf, buf_d, rd, wd_):
@@ -208,13 +209,6 @@
                         copy = pltpu.make_async_copy(rel, dest(out, j)(0, rel.shape[0]), rs.at[0])
                         copy.start()
                         copy.wait()
-
-        def other_kernel(dest, place_ref, got, _, out, buf, rs, ws):
-            me = where()
-
-            @pl.when(_any(me, sum(across, [])))
-            def _():
-                _one(got, [dest(out, j) for j in range(slots)], wants(scalars(place_ref), me, False), buf, rs, ws)
 
         def last_kernel(dest, place_ref, got, _, out, ws):
             want = wants(bits(place_ref), where(), False)
@@ -268,7 +262,7 @@
         def later(kernel, dest, got, out, cols, tile, rel_in=hbm):
             rel = permute(got, to_relay)
             return call(functools.partial(kernel, dest), shape(*out.shape), [smem, hbm, rel_in, hbm],
-                        ring(cols, tile), 3 * got.size * 2, {3: 0})(place, got, rel, out)
+                        ring(cols, tile), 3 * got.size * 2, {3: 0}, cols)(place, got, rel, out)
 
         w13 = later(both_kernel, lambda o, j: half(o, j, 0), got_g, w13, F, TILE)
         w13 = later(both_kernel, lambda o, j: half(o, j, 1), got_u, w13, F, TILE)
@@ -276,11 +270,10 @@
         w2 = later(first_kernel, lambda o, j: rows_of(o, j, BOTH_ROWS), got_d[1], w2, D, TILE // 2,
                    vmem)
         r = BOTH_ROWS
-        for i, got in enumerate(got_d[2:]):
-            kernel, ins, scratch = ((other_kernel, [smem, hbm, hbm], ring(D, TILE // 4, 1)) if i == 0 else
-                                    (last_kernel, [vmem, vmem, hbm], [pltpu.SemaphoreType.DMA((slots,))]))
-            w2 = call(functools.partial(kernel, lambda o, j, r=r: rows_of(o, j, r)),
-                      shape(*w2.shape), ins, scratch, 3 * got.size * 2, {2: 0})(place, got, w2)
+        for got in got_d[2:]:
+            w2 = call(functools.partial(last_kernel, lambda o, j, r=r: rows_of(o, j, r)),
+                      shape(*w2.shape), [vmem, vmem, hbm], [pltpu.SemaphoreType.DMA((slots,))],
+                      3 * got.size * 2, {2: 0})(place, got, w2)
             r += got.shape[0]
         return w13[None], w2[None]
 

time: 1010 us -> 1010 us (level)
  the two profiles are of different devices: /device:TPU:3 before, /device:TPU:1 now
where the time goes in v1:
time: 1010 us
  waiting for transfers between devices  783 us (78%)
  Pallas kernels  154 us (15%)
  starting transfers between devices  57.9 us (6%)
  local copies, waits for them, and re-layouts  10.5 us (1%)
    ppermute x14, waiting for transfers between devices, permute(): return lax.ppermute(x, axes, pairs)  783 us
    pallas_call x1, Pallas kernels, hand_over(): call(own_kernel, (shape(slots, D, 2 * F), shape(slots, F, D)), [smem] + [...  73.6 us
    ppermute x14, starting transfers between devices, permute(): return lax.ppermute(x, axes, pairs)  57.9 us
    pallas_call x4, Pallas kernels, later(): call(functools.partial(kernel, dest), shape(*out.shape), [smem, hbm, rel_...  55.7 us
    pallas_call x1, Pallas kernels, hand_over(): call(cut_kernel, [shape(n_exp, BOTH_ROWS, D), shape(F - BOTH_ROWS, D)] +...  20.2 us
  transfers between devices with their start and end apart: 14, of which 4 were waited for; matrix products, arithmetic and copies ran while one was open for 0% of the time, Pallas kernels for 13%

profile of v1, /device:TPU:1, one launch (start us, length us, event | category | flops | bytes accessed | tf_op | source)
XLA Modules:
  0.0 1005.9 jit_solution(11594640991601757014)
XLA Ops:
  0.6 3.9 collective-permute-start.2
  4.6 1.9 collective-permute-start
  7.2 20.2 %shard_map.62 = (bf16[2,768,4096]{2,1,0:T(8,128)(2,1)}, bf16[768,4096]{1,0:T(8,128)(2,1)S(1)}, bf16[656,4096]{1,0:T(8,128)(2,1)}, bf16[96,4096]{1,0:T(8,128)(2,1)S(1)}, bf16[16,4096]{1,0:T(8,128)(2,1)}) custom-call(s32[1,32]{1,0:T(1,128)S(1)} %copy-done.4, bf16[2,1536,4096]{2,1,0:T(8,128)(2,1)} %bitcast.6), custom_call_target="tpu_custom_call" | custom-call | bytes 50331648 | tf_op jit(solution)/shard_map/pallas_call | solution.py:254
  27.4 3.4 collective-permute-start.12
  30.8 1.9 collective-permute-start.10
  34.0 713.3 %collective-permute-done.10.got = bf16[768,4096]{1,0:T(8,128)(2,1)S(1)} collective-permute-done((bf16[768,4096]{1,0:T(8,128)(2,1)S(1)}, bf16[768,4096]{1,0:T(8,128)(2,1)S(1)}, u32[]{:S(2)}, u32[]{:S(2)}) %collective-permute-start.10) | collective-permute-done | bytes 6291488 | tf_op jit(solution)/shard_map/ppermute | solution.py:246
  749.0 2.6 copy-done
  752.9 5.4 collective-permute-done.11.rel
  758.3 2.6 copy-done.2
  762.2 19.6 %collective-permute-start.3 = (bf16[2,4096,1536]{2,1,0:T(8,128)(2,1)}, bf16[2,4096,1536]{2,1,0:T(8,128)(2,1)}, u32[]{:S(2)}, u32[]{:S(2)}) collective-permute-start(bf16[2,4096,1536]{2,1,0:T(8,128)(2,1)} %collective-permute-done.2.got), channel_id=1, source_target_pairs={{1,0},{3,2}} | collective-permute-start | bytes 75497480 | tf_op jit(solution)/shard_map/ppermute | solution.py:246
  781.8 9.5 collective-permute-start.1
  791.3 2.1 collective-permute-start.13
  793.4 3.4 collective-permute-start.9
  796.8 30.2 %collective-permute-done.6.cd = bf16[2,1536,4096]{2,1,0:T(8,128)(2,1)} collective-permute-done((bf16[2,1536,4096]{2,1,0:T(8,128)(2,1)}, bf16[2,1536,4096]{2,1,0:T(8,128)(2,1)}, u32[]{:S(2)}, u32[]{:S(2)}) %collective-permute-start.6) | collective-permute-done | bytes 25165856 | tf_op jit(solution)/shard_map/ppermute | solution.py:246
  827.0 3.4 collective-permute-start.8
  830.3 34.1 %collective-permute-done.13.rel = bf16[2,768,4096]{2,1,0:T(8,128)(2,1)S(1)} collective-permute-done((bf16[2,768,4096]{2,1,0:T(8,128)(2,1)S(1)}, bf16[2,768,4096]{2,1,0:T(8,128)(2,1)S(1)}, u32[]{:S(2)}, u32[]{:S(2)}) %collective-permute-start.13) | collective-permute-done | bytes 12582944 | tf_op jit(solution)/shard_map/ppermute | solution.py:246
  864.4 4.6 copy-done.7
  869.0 3.4 collective-permute-start.7
  872.3 73.6 %shard_map.59 = (bf16[4,4096,3072]{2,1,0:T(8,128)(2,1)}, bf16[4,1536,4096]{2,1,0:T(8,128)(2,1)}) custom-call(s32[1,32]{1,0:T(1,128)S(1)} %copy-done.4, bf16[2,4096,1536]{2,1,0:T(8,128)(2,1)} %bitcast.14, bf16[2,4096,1536]{2,1,0:T(8,128)(2,1)} %bitcast.11, bf16[2,1536,4096]{2,1,0:T(8,128)(2,1)} %bitcast.8, bf16[2,4096,1536]{2,1,0:T(8,128)(2,1)} %collective-permute-done.4.cg, ...), custom_call_target="tpu_custom_call" | custom-call | bytes 150994944 | tf_op jit(solution)/shard_map/pallas_call | solution.py:259
  946.0 10.7 %shard_map.63._ = bf16[4,1536,4096]{2,1,0:T(8,128)(2,1)} custom-call(s32[1,32]{1,0:T(1,128)S(1)} %copy-done.4, bf16[2,768,4096]{2,1,0:T(8,128)(2,1)S(1)} %collective-permute-done.12.got, bf16[2,768,4096]{2,1,0:T(8,128)(2,1)} %copy-done.7, bf16[4,1536,4096]{2,1,0:T(8,128)(2,1)} %get-tuple-element.15._), custom_call_target="tpu_custom_call", output_to_operand_aliasing={{}: (3, {})} | custom-call | bytes 37748736 | tf_op jit(solution)/shard_map/pallas_call | solution.py:264
  956.7 8.5 shard_map.64._
  965.2 2.7 shard_map.65._
  969.2 18.3 %shard_map.60._ = bf16[4,4096,3072]{2,1,0:T(8,128)(2,1)} custom-call(s32[1,32]{1,0:T(1,128)S(1)} %copy-done.5, bf16[2,4096,1536]{2,1,0:T(8,128)(2,1)} %collective-permute-done.2.got, bf16[2,4096,1536]{2,1,0:T(8,128)(2,1)} %collective-permute-done.3.rel, bf16[4,4096,3072]{2,1,0:T(8,128)(2,1)} %get-tuple-element.9._), custom_call_target="tpu_custom_call", output_to_operand_aliasing={{}: (3, {})} | custom-call | bytes 75497472 | tf_op jit(solution)/shard_map/pallas_call | solution.py:264
  987.6 18.3 %shard_map.61 = bf16[4,4096,3072]{2,1,0:T(8,128)(2,1)} custom-call(s32[1,32]{1,0:T(1,128)S(1)} %copy-done.5, bf16[2,4096,1536]{2,1,0:T(8,128)(2,1)} %collective-permute-done.got, bf16[2,4096,1536]{2,1,0:T(8,128)(2,1)} %collective-permute-done.1.rel, bf16[4,4096,3072]{2,1,0:T(8,128)(2,1)} %shard_map.60._), custom_call_target="tpu_custom_call", output_to_operand_aliasing={{}: (3, {})} | custom-call | bytes 75497472 | tf_op jit(solution)/shard_map/pallas_call | solution.py:264
  (29 shorter events, 7.5 us)
Async XLA Ops:
  0.6 761.6 %collective-permute-start.2 = (bf16[2,4096,1536]{2,1,0:T(8,128)(2,1)}, bf16[2,4096,1536]{2,1,0:T(8,128)(2,1)}, u32[]{:S(2)}, u32[]{:S(2)}) collective-permute-start(bf16[2,4096,1536]{2,1,0:T(8,128)(2,1)} %bitcast.12), channel_id=1, source_target_pairs={{3,1},{1,3},{6,4},{4,6}} | collective-permute-start | bytes 75497480 | tf_op jit(solution)/shard_map/ppermute | solution.py:246
  4.6 777.2 %collective-permute-start = (bf16[2,4096,1536]{2,1,0:T(8,128)(2,1)}, bf16[2,4096,1536]{2,1,0:T(8,128)(2,1)}, u32[]{:S(2)}, u32[]{:S(2)}) collective-permute-start(bf16[2,4096,1536]{2,1,0:T(8,128)(2,1)} %bitcast.9), channel_id=1, source_target_pairs={{3,1},{1,3},{6,4},{4,6}} | collective-permute-start | bytes 75497480 | tf_op jit(solution)/shard_map/ppermute | solution.py:246
  6.5 0.7 copy-start.4
  27.4 724.2 %collective-permute-start.12 = (bf16[2,768,4096]{2,1,0:T(8,128)(2,1)}, bf16[2,768,4096]{2,1,0:T(8,128)(2,1)S(1)}, u32[]{:S(2)}, u32[]{:S(2)}) collective-permute-start(bf16[2,768,4096]{2,1,0:T(8,128)(2,1)} %get-tuple-element.14), channel_id=1, source_target_pairs={{3,1},{1,3},{6,4},{4,6}} | collective-permute-start | bytes 37748744 | tf_op jit(solution)/shard_map/ppermute | solution.py:246
  30.8 716.5 %collective-permute-start.10 = (bf16[768,4096]{1,0:T(8,128)(2,1)S(1)}, bf16[768,4096]{1,0:T(8,128)(2,1)S(1)}, u32[]{:S(2)}, u32[]{:S(2)}) collective-permute-start(bf16[768,4096]{1,0:T(8,128)(2,1)S(1)} %get-tuple-element.13), channel_id=1, source_target_pairs={{3,1},{1,3},{6,4},{4,6}} | collective-permute-start | bytes 18874376 | tf_op jit(solution)/shard_map/ppermute | solution.py:246
  32.7 758.6 %collective-permute-start.4 = (bf16[2,4096,1536]{2,1,0:T(8,128)(2,1)}, bf16[2,4096,1536]{2,1,0:T(8,128)(2,1)}, u32[]{:S(2)}, u32[]{:S(2)}) collective-permute-start(bf16[2,4096,1536]{2,1,0:T(8,128)(2,1)} %bitcast.13), channel_id=1, source_target_pairs={{0,1},{2,3}} | collective-permute-start | bytes 75497480 | tf_op jit(solution)/shard_map/ppermute | solution.py:246
  747.3 11.1 %collective-permute-start.11 = (bf16[768,4096]{1,0:T(8,128)(2,1)S(1)}, bf16[768,4096]{1,0:T(8,128)(2,1)S(1)}, u32[]{:S(2)}, u32[]{:S(2)}) collective-permute-start(bf16[768,4096]{1,0:T(8,128)(2,1)S(1)} %collective-permute-done.10.got), channel_id=1, source_target_pairs={{1,0},{3,2}} | collective-permute-start | bytes 18874376 | tf_op jit(solution)/shard_map/ppermute | solution.py:246
  749.0 2.6 copy-start
  751.6 41.8 %collective-permute-start.5 = (bf16[2,4096,1536]{2,1,0:T(8,128)(2,1)}, bf16[2,4096,1536]{2,1,0:T(8,128)(2,1)S(1)}, u32[]{:S(2)}, u32[]{:S(2)}) collective-permute-start(bf16[2,4096,1536]{2,1,0:T(8,128)(2,1)} %bitcast.10), channel_id=1, source_target_pairs={{0,1},{2,3}} | collective-permute-start | bytes 75497480 | tf_op jit(solution)/shard_map/ppermute | solution.py:246
  758.3 2.6 copy-start.2
  760.9 66.0 %collective-permute-start.6 = (bf16[2,1536,4096]{2,1,0:T(8,128)(2,1)}, bf16[2,1536,4096]{2,1,0:T(8,128)(2,1)}, u32[]{:S(2)}, u32[]{:S(2)}) collective-permute-start(bf16[2,1536,4096]{2,1,0:T(8,128)(2,1)} %bitcast.7), channel_id=1, source_target_pairs={{0,1},{2,3}} | collective-permute-start | bytes 75497480 | tf_op jit(solution)/shard_map/ppermute | solution.py:246
  762.2 207.0 %collective-permute-start.3 = (bf16[2,4096,1536]{2,1,0:T(8,128)(2,1)}, bf16[2,4096,1536]{2,1,0:T(8,128)(2,1)}, u32[]{:S(2)}, u32[]{:S(2)}) collective-permute-start(bf16[2,4096,1536]{2,1,0:T(8,128)(2,1)} %collective-permute-done.2.got), channel_id=1, source_target_pairs={{1,0},{3,2}} | collective-permute-start | bytes 75497480 | tf_op jit(solution)/shard_map/ppermute | solution.py:246
  781.8 205.8 %collective-permute-start.1 = (bf16[2,4096,1536]{2,1,0:T(8,128)(2,1)}, bf16[2,4096,1536]{2,1,0:T(8,128)(2,1)}, u32[]{:S(2)}, u32[]{:S(2)}) collective-permute-start(bf16[2,4096,1536]{2,1,0:T(8,128)(2,1)} %collective-permute-done.got), channel_id=1, source_target_pairs={{1,0},{3,2}} | collective-permute-start | bytes 75497480 | tf_op jit(solution)/shard_map/ppermute | solution.py:246
  791.3 73.1 %collective-permute-start.13 = (bf16[2,768,4096]{2,1,0:T(8,128)(2,1)S(1)}, bf16[2,768,4096]{2,1,0:T(8,128)(2,1)S(1)}, u32[]{:S(2)}, u32[]{:S(2)}) collective-permute-start(bf16[2,768,4096]{2,1,0:T(8,128)(2,1)S(1)} %collective-permute-done.12.got), channel_id=1, source_target_pairs={{1,0},{3,2}} | collective-permute-start | bytes 37748744 | tf_op jit(solution)/shard_map/ppermute | solution.py:246
  793.4 33.6 %copy-start.6 = (bf16[2,4096,1536]{2,1,0:T(8,128)(2,1)}, bf16[2,4096,1536]{2,1,0:T(8,128)(2,1)S(1)}, u32[]{:S(2)}) copy-start(bf16[2,4096,1536]{2,1,0:T(8,128)(2,1)S(1)} %collective-permute-done.5.cu) | copy-start | bytes 75497472
  793.4 171.7 %collective-permute-start.9 = (bf16[656,4096]{1,0:T(8,128)(2,1)}, bf16[656,4096]{1,0:T(8,128)(2,1)}, u32[]{:S(2)}, u32[]{:S(2)}) collective-permute-start(bf16[656,4096]{1,0:T(8,128)(2,1)} %get-tuple-element.12), channel_id=1, source_target_pairs={{3,1},{1,3},{6,4},{4,6}} | collective-permute-start | bytes 16121864 | tf_op jit(solution)/shard_map/ppermute | solution.py:246
  827.0 140.9 %collective-permute-start.8 = (bf16[96,4096]{1,0:T(8,128)(2,1)S(1)}, bf16[96,4096]{1,0:T(8,128)(2,1)S(1)}, u32[]{:S(2)}, u32[]{:S(2)}) collective-permute-start(bf16[96,4096]{1,0:T(8,128)(2,1)S(1)} %get-tuple-element.11), channel_id=1, source_target_pairs={{3,1},{1,3},{6,4},{4,6}} | collective-permute-start | bytes 2359304 | tf_op jit(solution)/shard_map/ppermute | solution.py:246
  864.4 4.6 copy-start.7
  869.0 99.1 %collective-permute-start.7 = (bf16[16,4096]{1,0:T(8,128)(2,1)}, bf16[16,4096]{1,0:T(8,128)(2,1)}, u32[]{:S(2)}, u32[]{:S(2)}) collective-permute-start(bf16[16,4096]{1,0:T(8,128)(2,1)} %get-tuple-element.10), channel_id=1, source_target_pairs={{3,1},{1,3},{6,4},{4,6}} | collective-permute-start | bytes 393224 | tf_op jit(solution)/shard_map/ppermute | solution.py:246
  946.0 10.7 %copy-start.1 = (bf16[768,4096]{1,0:T(8,128)(2,1)S(1)}, bf16[768,4096]{1,0:T(8,128)(2,1)}, u32[]{:S(2)}) copy-start(bf16[768,4096]{1,0:T(8,128)(2,1)} %copy-done) | copy-start | bytes 18874372
  946.0 10.7 %copy-start.3 = (bf16[768,4096]{1,0:T(8,128)(2,1)S(1)}, bf16[768,4096]{1,0:T(8,128)(2,1)}, u32[]{:S(2)}) copy-start(bf16[768,4096]{1,0:T(8,128)(2,1)} %copy-done.2) | copy-start | bytes 18874372
  968.1 1.1 copy-start.5

commit v2 on v1

--- a/solution.py
+++ b/solution.py
@@ -12,8 +12,8 @@
 NBUF = 4
 VMEM_LIMIT = 36 * 1024 * 1024
 VMEM_LIMIT_WIDE = 44 * 1024 * 1024
-BOTH_ROWS = 768
-LAST_ROWS = (656, 96, 16)
+BOTH_ROWS = 960
+LAST_ROWS = (464, 96, 16)
 
 
 def _shard(dp, ep, slots, a, g, j):
@@ -109,6 +109,9 @@
         to_x = [(n ^ 2, n) for n in sorted(set(sum(across, [])) | {m ^ 1 for m in sum(relayed, [])})]
         to_core = [(n ^ 1, n) for n in sorted(set(sum(beside, [])))]
         to_relay = [(n ^ 1, n) for n in sorted(set(sum(relayed, [])))]
+        last_from = {n: n ^ 2 | 1 for _, n in to_x}
+        lent = [(n ^ 2, m) for n, m in last_from.items() if m != n ^ 2]
+        to_last = [(m, n) for n, m in last_from.items()]
 
         def ring(cols, tile, experts=n_exp):
             return [pltpu.VMEM((NBUF, experts, tile, cols), jnp.bfloat16),
@@ -126,7 +129,7 @@
         def picks(place_ref, me):
             return [lax.rem(place_ref[0, me * slots + j], n_exp) for j in range(slots)]
 
-        def early(pick, me, flip):
+        def early(pick, me, actor):
             e = me * 0
             for _, n in to_x:
                 on = [j for j in range(slots) if n ^ 1 in relayed[j]]
@@ -135,7 +138,7 @@
                     first = pick(n ^ 1, on[0])
                 else:
                     first = jnp.where(2 * sum(pick(n, j) for j in here) > len(here), 1, 0)
-                e = jnp.where(me == n ^ flip, first, e)
+                e = jnp.where(me == actor(n), first, e)
             return e
 
         def scalars(place_ref):
@@ -191,7 +194,7 @@
                         _one(rel.at[e[j]], [dest(out, j)], [True], buf, rs, ws)
 
         def wants(pick, me, first):
-            a = early(pick, me, 0)
+            a = early(pick, me, lambda n: n)
             return [jnp.logical_and(_any(me, across[j]), (pick(me, j) == a) == first) if across[j] else None
                     for j in range(slots)]
 
@@ -219,18 +222,10 @@
                         def _():
                             act(pltpu.make_async_copy(got, dest(out, j)(0, got.shape[0]), ws.at[j]))
 
-        def cut_kernel(place_ref, d, both, *rest):
-            pieces, (buf, rs, ws) = rest[:-3], rest[-3:]
-            e = early(scalars(place_ref), where(), 2)
-            tile = buf.shape[2]
-            steps = [(d.at[x, pl.ds(r, n)], both.at[x, pl.ds(r, n)], n)
-                     for x in range(n_exp) for r, n in _tiles(BOTH_ROWS, tile)]
-            first = BOTH_ROWS
-            for i, o in enumerate(pieces):
-                x = e if i == 0 else 1 - e
-                for r, n in _tiles(o.shape[0], tile):
-                    steps.append((d.at[x, pl.ds(first + r, n)], o.at[pl.ds(r, n)], n))
-                first = BOTH_ROWS if i == 0 else first + o.shape[0]
+        def cut(pieces, buf, rs, ws):
+            steps = []
+            for src, dst in pieces:
+                steps += [(src.at[pl.ds(r, n)], dst.at[pl.ds(r, n)], n) for r, n in _tiles(dst.shape[0], buf.shape[2])]
 
             def read(t):
                 src, _, n = steps[t]
@@ -242,6 +237,24 @@
 
             _stream(len(steps), read, writes)
 
+        def cut_kernel(place_ref, d, both, first, buf, rs, ws):
+            e = early(scalars(place_ref), where(), lambda n: n ^ 2)
+            cut([(d.at[x, pl.ds(0, BOTH_ROWS)], both.at[x]) for x in range(n_exp)]
+                + [(d.at[e, pl.ds(BOTH_ROWS, F - BOTH_ROWS)], first)], buf, rs, ws)
+
+        def cut_last_kernel(place_ref, d, cd, *rest):
+            outs, (buf, rs, ws) = rest[:-3], rest[-3:]
+            me = where()
+            x = 1 - early(scalars(place_ref), me, lambda n: last_from[n])
+            for src, mine in ((d, [m for m, n in to_last if m == n ^ 2]), (cd, [m for _, m in lent])):
+                @pl.when(_any(me, mine))
+                def _():
+                    pieces, r = [], BOTH_ROWS
+                    for o in outs:
+                        pieces.append((src.at[x, pl.ds(r, o.shape[0])], o))
+                        r += o.shape[0]
+                    cut(pieces, buf, rs, ws)
+
         def permute(x, pairs):
             return lax.ppermute(x, axes, pairs)
 
@@ -251,11 +264,12 @@
         block = wg.size * wg.dtype.itemsize
         got_g = permute(wg, to_x)
         got_u = permute(wu, to_x)
-        cuts = call(cut_kernel,
-                    [shape(n_exp, BOTH_ROWS, D), shape(F - BOTH_ROWS, D)] + [shape(n, D) for n in LAST_ROWS],
+        cuts = call(cut_kernel, [shape(n_exp, BOTH_ROWS, D), shape(F - BOTH_ROWS, D)],
                     [smem, hbm], ring(D, TILE // 2, 1), 2 * block)(place, wd)
-        got_d = [permute(c, to_x) for c in cuts]
-        side = [permute(w, to_core) for w in (wg, wu, wd)]
+        side = [permute(w, to_core + (lent if i == 2 else [])) for i, w in enumerate((wg, wu, wd))]
+        lasts = call(cut_last_kernel, [shape(n, D) for n in LAST_ROWS],
+                     [smem, hbm, hbm], ring(D, TILE // 2, 1), 2 * block)(place, wd, side[2])
+        got_d = [permute(c, to_x if i < 2 else to_last) for i, c in enumerate(cuts + lasts)]
         w13, w2 = call(own_kernel, (shape(slots, D, 2 * F), shape(slots, F, D)),
                        [smem] + [hbm] * 6, ring(F, TILE) + ring(D, TILE // 4), 6 * block)(place, wg, wu, wd, *side)
 

time: 1010 us -> 1030 us (1.020)
  waiting for transfers between devices: 783 us -> 798 us
  starting transfers between devices: 57.9 us -> 70.7 us
    ppermute x14, waiting for transfers between devices: 783 us -> 798 us  [permute(): return lax.ppermute(x, axes, pairs)]
    ppermute x14, starting transfers between devices: 57.9 us -> 70.7 us  [permute(): return lax.ppermute(x, axes, pairs)]
    pallas_call x1 -> x2, Pallas kernels: 20.2 us -> 23.9 us  [the longest x1 16.2 us: hand_over(): call(cut_kernel, [shape(n_exp, BOTH_ROWS, D), shape(F - BOTH_ROWS, D)], [...]
where the time goes in v2:
time: 1030 us
  waiting for transfers between devices  798 us (77%)
  Pallas kernels  157 us (15%)
  starting transfers between devices  70.7 us (7%)
    ppermute x14, waiting for transfers between devices, permute(): return lax.ppermute(x, axes, pairs)  798 us
    pallas_call x1, Pallas kernels, hand_over(): call(own_kernel, (shape(slots, D, 2 * F), shape(slots, F, D)), [smem] + [...  73.6 us
    ppermute x14, starting transfers between devices, permute(): return lax.ppermute(x, axes, pairs)  70.7 us
    pallas_call x4, Pallas kernels, later(): call(functools.partial(kernel, dest), shape(*out.shape), [smem, hbm, rel_...  57.1 us
  transfers between devices with their start and end apart: 14, of which 4 were waited for; matrix products, arithmetic and copies ran while one was open for 0% of the time, Pallas kernels for 13%

profile of v2, /device:TPU:1, one launch (start us, length us, event | category | flops | bytes accessed | tf_op | source)
XLA Modules:
  0.0 1029.5 jit_solution(10103351072349547972)
XLA Ops:
  0.6 3.9 collective-permute-start.2
  4.6 1.9 collective-permute-start
  7.2 16.2 %shard_map.63 = (bf16[2,960,4096]{2,1,0:T(8,128)(2,1)}, bf16[576,4096]{1,0:T(8,128)(2,1)S(1)}) custom-call(s32[1,32]{1,0:T(1,128)S(1)} %copy-done.2, bf16[2,1536,4096]{2,1,0:T(8,128)(2,1)} %bitcast.6), custom_call_target="tpu_custom_call" | custom-call | bytes 50331648 | tf_op jit(solution)/shard_map/pallas_call | solution.py:267
  23.4 3.4 collective-permute-start.12
  28.1 1.9 collective-permute-start.10
  30.0 734.1 %collective-permute-done.10.got = bf16[576,4096]{1,0:T(8,128)(2,1)S(1)} collective-permute-done((bf16[576,4096]{1,0:T(8,128)(2,1)S(1)}, bf16[576,4096]{1,0:T(8,128)(2,1)S(1)}, u32[]{:S(2)}, u32[]{:S(2)}) %collective-permute-start.10) | collective-permute-done | bytes 4718624 | tf_op jit(solution)/shard_map/ppermute | solution.py:259
  764.1 1.6 collective-permute-start.11
  765.7 7.2 collective-permute-done.11.rel
  772.9 2.1 copy-done
  777.7 27.8 %collective-permute-start.3 = (bf16[2,4096,1536]{2,1,0:T(8,128)(2,1)}, bf16[2,4096,1536]{2,1,0:T(8,128)(2,1)}, u32[]{:S(2)}, u32[]{:S(2)}) collective-permute-start(bf16[2,4096,1536]{2,1,0:T(8,128)(2,1)} %collective-permute-done.2.got), channel_id=1, source_target_pairs={{1,0},{3,2}} | collective-permute-start | bytes 75497480 | tf_op jit(solution)/shard_map/ppermute | solution.py:259
  805.5 9.5 collective-permute-start.1
  815.0 6.7 collective-permute-start.13
  821.7 7.7 shard_map.62
  829.4 3.4 collective-permute-start.9
  832.8 17.7 %collective-permute-done.5.cu = bf16[2,4096,1536]{2,1,0:T(8,128)(2,1)} collective-permute-done((bf16[2,4096,1536]{2,1,0:T(8,128)(2,1)}, bf16[2,4096,1536]{2,1,0:T(8,128)(2,1)}, u32[]{:S(2)}, u32[]{:S(2)}) %collective-permute-start.5) | collective-permute-done | bytes 25165856 | tf_op jit(solution)/shard_map/ppermute | solution.py:259
  850.4 3.4 collective-permute-start.8
  853.8 39.0 %collective-permute-done.13.rel = bf16[2,960,4096]{2,1,0:T(8,128)(2,1)} collective-permute-done((bf16[2,960,4096]{2,1,0:T(8,128)(2,1)S(1)}, bf16[2,960,4096]{2,1,0:T(8,128)(2,1)}, u32[]{:S(2)}, u32[]{:S(2)}) %collective-permute-start.13) | collective-permute-done | bytes 15728672 | tf_op jit(solution)/shard_map/ppermute | solution.py:259
  892.7 3.4 collective-permute-start.7
  896.1 73.6 %shard_map.59 = (bf16[4,4096,3072]{2,1,0:T(8,128)(2,1)}, bf16[4,1536,4096]{2,1,0:T(8,128)(2,1)}) custom-call(s32[1,32]{1,0:T(1,128)S(1)} %copy-done.2, bf16[2,4096,1536]{2,1,0:T(8,128)(2,1)} %bitcast.15, bf16[2,4096,1536]{2,1,0:T(8,128)(2,1)} %bitcast.12, bf16[2,1536,4096]{2,1,0:T(8,128)(2,1)} %bitcast.9, bf16[2,4096,1536]{2,1,0:T(8,128)(2,1)} %collective-permute-done.4.cg, ...), custom_call_target="tpu_custom_call" | custom-call | bytes 150994944 | tf_op jit(solution)/shard_map/pallas_call | solution.py:273
  969.7 13.2 %shard_map.64._ = bf16[4,1536,4096]{2,1,0:T(8,128)(2,1)} custom-call(s32[1,32]{1,0:T(1,128)S(1)} %copy-done.2, bf16[2,960,4096]{2,1,0:T(8,128)(2,1)S(1)} %collective-permute-done.12.got, bf16[2,960,4096]{2,1,0:T(8,128)(2,1)} %collective-permute-done.13.rel, bf16[4,1536,4096]{2,1,0:T(8,128)(2,1)} %get-tuple-element.15._), custom_call_target="tpu_custom_call", output_to_operand_aliasing={{}: (3, {})} | custom-call | bytes 47185920 | tf_op jit(solution)/shard_map/pallas_call | solution.py:278
  982.9 7.3 shard_map.65._
  990.5 1.3 shard_map.67._
  992.9 18.3 %shard_map.60._ = bf16[4,4096,3072]{2,1,0:T(8,128)(2,1)} custom-call(s32[1,32]{1,0:T(1,128)S(1)} %copy-done.3, bf16[2,4096,1536]{2,1,0:T(8,128)(2,1)} %collective-permute-done.2.got, bf16[2,4096,1536]{2,1,0:T(8,128)(2,1)} %collective-permute-done.3.rel, bf16[4,4096,3072]{2,1,0:T(8,128)(2,1)} %get-tuple-element.9._), custom_call_target="tpu_custom_call", output_to_operand_aliasing={{}: (3, {})} | custom-call | bytes 75497472 | tf_op jit(solution)/shard_map/pallas_call | solution.py:278
  1011.2 18.3 %shard_map.61 = bf16[4,4096,3072]{2,1,0:T(8,128)(2,1)} custom-call(s32[1,32]{1,0:T(1,128)S(1)} %copy-done.3, bf16[2,4096,1536]{2,1,0:T(8,128)(2,1)} %collective-permute-done.got, bf16[2,4096,1536]{2,1,0:T(8,128)(2,1)} %collective-permute-done.1.rel, bf16[4,4096,3072]{2,1,0:T(8,128)(2,1)} %shard_map.60._), custom_call_target="tpu_custom_call", output_to_operand_aliasing={{}: (3, {})} | custom-call | bytes 75497472 | tf_op jit(solution)/shard_map/pallas_call | solution.py:278
  (22 shorter events, 5.8 us)
Async XLA Ops:
  0.6 777.0 %collective-permute-start.2 = (bf16[2,4096,1536]{2,1,0:T(8,128)(2,1)}, bf16[2,4096,1536]{2,1,0:T(8,128)(2,1)}, u32[]{:S(2)}, u32[]{:S(2)}) collective-permute-start(bf16[2,4096,1536]{2,1,0:T(8,128)(2,1)} %bitcast.13), channel_id=1, source_target_pairs={{3,1},{1,3},{6,4},{4,6}} | collective-permute-start | bytes 75497480 | tf_op jit(solution)/shard_map/ppermute | solution.py:259
  4.6 800.9 %collective-permute-start = (bf16[2,4096,1536]{2,1,0:T(8,128)(2,1)}, bf16[2,4096,1536]{2,1,0:T(8,128)(2,1)}, u32[]{:S(2)}, u32[]{:S(2)}) collective-permute-start(bf16[2,4096,1536]{2,1,0:T(8,128)(2,1)} %bitcast.10), channel_id=1, source_target_pairs={{3,1},{1,3},{6,4},{4,6}} | collective-permute-start | bytes 75497480 | tf_op jit(solution)/shard_map/ppermute | solution.py:259
  6.5 0.7 copy-start.2
  23.4 752.9 %collective-permute-start.12 = (bf16[2,960,4096]{2,1,0:T(8,128)(2,1)}, bf16[2,960,4096]{2,1,0:T(8,128)(2,1)S(1)}, u32[]{:S(2)}, u32[]{:S(2)}) collective-permute-start(bf16[2,960,4096]{2,1,0:T(8,128)(2,1)} %get-tuple-element.14), channel_id=1, source_target_pairs={{3,1},{1,3},{6,4},{4,6}} | collective-permute-start | bytes 47185928 | tf_op jit(solution)/shard_map/ppermute | solution.py:259
  26.8 788.2 %collective-permute-start.6 = (bf16[2,1536,4096]{2,1,0:T(8,128)(2,1)}, bf16[2,1536,4096]{2,1,0:T(8,128)(2,1)}, u32[]{:S(2)}, u32[]{:S(2)}) collective-permute-start(bf16[2,1536,4096]{2,1,0:T(8,128)(2,1)} %bitcast.7), channel_id=1, source_target_pairs={{0,1},{2,3},{6,7},{4,5}} | collective-permute-start | bytes 75497480 | tf_op jit(solution)/shard_map/ppermute | solution.py:259
  28.1 736.0 %collective-permute-start.10 = (bf16[576,4096]{1,0:T(8,128)(2,1)S(1)}, bf16[576,4096]{1,0:T(8,128)(2,1)S(1)}, u32[]{:S(2)}, u32[]{:S(2)}) collective-permute-start(bf16[576,4096]{1,0:T(8,128)(2,1)S(1)} %get-tuple-element.13), channel_id=1, source_target_pairs={{3,1},{1,3},{6,4},{4,6}} | collective-permute-start | bytes 14155784 | tf_op jit(solution)/shard_map/ppermute | solution.py:259
  764.1 8.8 collective-permute-start.11
  772.9 2.1 copy-start
  775.0 54.3 %collective-permute-start.4 = (bf16[2,4096,1536]{2,1,0:T(8,128)(2,1)}, bf16[2,4096,1536]{2,1,0:T(8,128)(2,1)}, u32[]{:S(2)}, u32[]{:S(2)}) collective-permute-start(bf16[2,4096,1536]{2,1,0:T(8,128)(2,1)} %bitcast.14), channel_id=1, source_target_pairs={{0,1},{2,3}} | collective-permute-start | bytes 75497480 | tf_op jit(solution)/shard_map/ppermute | solution.py:259
  776.3 74.1 %collective-permute-start.5 = (bf16[2,4096,1536]{2,1,0:T(8,128)(2,1)}, bf16[2,4096,1536]{2,1,0:T(8,128)(2,1)}, u32[]{:S(2)}, u32[]{:S(2)}) collective-permute-start(bf16[2,4096,1536]{2,1,0:T(8,128)(2,1)} %bitcast.11), channel_id=1, source_target_pairs={{0,1},{2,3}} | collective-permute-start | bytes 75497480 | tf_op jit(solution)/shard_map/ppermute | solution.py:259
  777.7 215.3 %collective-permute-start.3 = (bf16[2,4096,1536]{2,1,0:T(8,128)(2,1)}, bf16[2,4096,1536]{2,1,0:T(8,128)(2,1)}, u32[]{:S(2)}, u32[]{:S(2)}) collective-permute-start(bf16[2,4096,1536]{2,1,0:T(8,128)(2,1)} %collective-permute-done.2.got), channel_id=1, source_target_pairs={{1,0},{3,2}} | collective-permute-start | bytes 75497480 | tf_op jit(solution)/shard_map/ppermute | solution.py:259
  805.5 205.8 %collective-permute-start.1 = (bf16[2,4096,1536]{2,1,0:T(8,128)(2,1)}, bf16[2,4096,1536]{2,1,0:T(8,128)(2,1)}, u32[]{:S(2)}, u32[]{:S(2)}) collective-permute-start(bf16[2,4096,1536]{2,1,0:T(8,128)(2,1)} %collective-permute-done.got), channel_id=1, source_target_pairs={{1,0},{3,2}} | collective-permute-start | bytes 75497480 | tf_op jit(solution)/shard_map/ppermute | solution.py:259
  815.0 77.7 %collective-permute-start.13 = (bf16[2,960,4096]{2,1,0:T(8,128)(2,1)S(1)}, bf16[2,960,4096]{2,1,0:T(8,128)(2,1)}, u32[]{:S(2)}, u32[]{:S(2)}) collective-permute-start(bf16[2,960,4096]{2,1,0:T(8,128)(2,1)S(1)} %collective-permute-done.12.got), channel_id=1, source_target_pairs={{1,0},{3,2}} | collective-permute-start | bytes 47185928 | tf_op jit(solution)/shard_map/ppermute | solution.py:259
  829.4 160.8 %collective-permute-start.9 = (bf16[464,4096]{1,0:T(8,128)(2,1)}, bf16[464,4096]{1,0:T(8,128)(2,1)S(1)}, u32[]{:S(2)}, u32[]{:S(2)}) collective-permute-start(bf16[464,4096]{1,0:T(8,128)(2,1)} %get-tuple-element.12), channel_id=1, source_target_pairs={{3,1},{1,3},{7,4},{5,6}} | collective-permute-start | bytes 11403272 | tf_op jit(solution)/shard_map/ppermute | solution.py:259
  850.4 140.0 %collective-permute-start.8 = (bf16[96,4096]{1,0:T(8,128)(2,1)}, bf16[96,4096]{1,0:T(8,128)(2,1)}, u32[]{:S(2)}, u32[]{:S(2)}) collective-permute-start(bf16[96,4096]{1,0:T(8,128)(2,1)} %get-tuple-element.11), channel_id=1, source_target_pairs={{3,1},{1,3},{7,4},{5,6}} | collective-permute-start | bytes 2359304 | tf_op jit(solution)/shard_map/ppermute | solution.py:259
  892.7 99.1 %collective-permute-start.7 = (bf16[16,4096]{1,0:T(8,128)(2,1)}, bf16[16,4096]{1,0:T(8,128)(2,1)}, u32[]{:S(2)}, u32[]{:S(2)}) collective-permute-start(bf16[16,4096]{1,0:T(8,128)(2,1)} %get-tuple-element.10), channel_id=1, source_target_pairs={{3,1},{1,3},{7,4},{5,6}} | collective-permute-start | bytes 393224 | tf_op jit(solution)/shard_map/ppermute | solution.py:259
  969.7 13.2 %copy-start.1 = (bf16[576,4096]{1,0:T(8,128)(2,1)S(1)}, bf16[576,4096]{1,0:T(8,128)(2,1)}, u32[]{:S(2)}) copy-start(bf16[576,4096]{1,0:T(8,128)(2,1)} %copy-done) | copy-start | bytes 14155780
  991.8 1.1 copy-start.3

commit v3 on v1

--- a/solution.py
+++ b/solution.py
@@ -13,7 +13,7 @@
 VMEM_LIMIT = 36 * 1024 * 1024
 VMEM_LIMIT_WIDE = 44 * 1024 * 1024
 BOTH_ROWS = 768
-LAST_ROWS = (656, 96, 16)
+LAST = ((1504, 1536, 0, 512, True), (768, 1424, 0, 4096, False), (1424, 1504, 0, 4096, False), (1504, 1536, 512, 4096, False))
 
 
 def _shard(dp, ep, slots, a, g, j):
@@ -109,6 +109,7 @@
         to_x = [(n ^ 2, n) for n in sorted(set(sum(across, [])) | {m ^ 1 for m in sum(relayed, [])})]
         to_core = [(n ^ 1, n) for n in sorted(set(sum(beside, [])))]
         to_relay = [(n ^ 1, n) for n in sorted(set(sum(relayed, [])))]
+        to_block = [(m if n ^ 1 in sum(relayed, []) else m ^ ep, n) for m, n in to_x]
 
         def ring(cols, tile, experts=n_exp):
             return [pltpu.VMEM((NBUF, experts, tile, cols), jnp.bfloat16),
@@ -126,7 +127,7 @@
         def picks(place_ref, me):
             return [lax.rem(place_ref[0, me * slots + j], n_exp) for j in range(slots)]
 
-        def early(pick, me, flip):
+        def early(pick, me, actors):
             e = me * 0
             for _, n in to_x:
                 on = [j for j in range(slots) if n ^ 1 in relayed[j]]
@@ -135,7 +136,7 @@
                     first = pick(n ^ 1, on[0])
                 else:
                     first = jnp.where(2 * sum(pick(n, j) for j in here) > len(here), 1, 0)
-                e = jnp.where(me == n ^ flip, first, e)
+                e = jnp.where(_any(me, actors(n)), first, e)
             return e
 
         def scalars(place_ref):
@@ -191,7 +192,7 @@
                         _one(rel.at[e[j]], [dest(out, j)], [True], buf, rs, ws)
 
         def wants(pick, me, first):
-            a = early(pick, me, 0)
+            a = early(pick, me, lambda n: [n])
             return [jnp.logical_and(_any(me, across[j]), (pick(me, j) == a) == first) if across[j] else None
                     for j in range(slots)]
 
@@ -217,28 +218,27 @@
                     if want[j] is not None:
                         @pl.when(want[j])
                         def _():
-                            act(pltpu.make_async_copy(got, dest(out, j)(0, got.shape[0]), ws.at[j]))
+                            act(pltpu.make_async_copy(got, dest(out, j), ws.at[j]))
 
         def cut_kernel(place_ref, d, both, *rest):
             pieces, (buf, rs, ws) = rest[:-3], rest[-3:]
-            e = early(scalars(place_ref), where(), 2)
+            e = early(scalars(place_ref), where(), lambda n: [m for m, r in to_x + to_block if r == n])
             tile = buf.shape[2]
             steps = [(d.at[x, pl.ds(r, n)], both.at[x, pl.ds(r, n)], n)
                      for x in range(n_exp) for r, n in _tiles(BOTH_ROWS, tile)]
-            first = BOTH_ROWS
-            for i, o in enumerate(pieces):
-                x = e if i == 0 else 1 - e
-                for r, n in _tiles(o.shape[0], tile):
-                    steps.append((d.at[x, pl.ds(first + r, n)], o.at[pl.ds(r, n)], n))
-                first = BOTH_ROWS if i == 0 else first + o.shape[0]
+            rects = [(e, BOTH_ROWS, F, 0, D)] + [(1 - e, r0, r1, c0, c1) for r0, r1, c0, c1, _ in LAST]
+            for (x, r0, r1, c0, c1), o in zip(rects, pieces):
+                for r, n in _tiles(r1 - r0, tile):
+                    steps.append((d.at[x, pl.ds(r0 + r, n), pl.ds(c0, c1 - c0)], o.at[pl.ds(r, n)], n))
+
+            def part(t):
+                return buf.at[t % NBUF, 0, pl.ds(0, steps[t][2]), pl.ds(0, steps[t][0].shape[1])]
 
             def read(t):
-                src, _, n = steps[t]
-                return pltpu.make_async_copy(src, buf.at[t % NBUF, 0, pl.ds(0, n)], rs.at[t % NBUF])
+                return pltpu.make_async_copy(steps[t][0], part(t), rs.at[t % NBUF])
 
             def writes(t, act):
-                _, dst, n = steps[t]
-                act(pltpu.make_async_copy(buf.at[t % NBUF, 0, pl.ds(0, n)], dst, ws.at[t % NBUF, 0]))
+                act(pltpu.make_async_copy(part(t), steps[t][1], ws.at[t % NBUF, 0]))
 
             _stream(len(steps), read, writes)
 
@@ -252,9 +252,9 @@
         got_g = permute(wg, to_x)
         got_u = permute(wu, to_x)
         cuts = call(cut_kernel,
-                    [shape(n_exp, BOTH_ROWS, D), shape(F - BOTH_ROWS, D)] + [shape(n, D) for n in LAST_ROWS],
+                    [shape(n_exp, BOTH_ROWS, D), shape(F - BOTH_ROWS, D)] + [shape(r1 - r0, c1 - c0) for r0, r1, c0, c1, _ in LAST],
                     [smem, hbm], ring(D, TILE // 2, 1), 2 * block)(place, wd)
-        got_d = [permute(c, to_x) for c in cuts]
+        got_d = [permute(c, to_block if i > 1 and LAST[i - 2][4] else to_x) for i, c in enumerate(cuts)]
         side = [permute(w, to_core) for w in (wg, wu, wd)]
         w13, w2 = call(own_kernel, (shape(slots, D, 2 * F), shape(slots, F, D)),
                        [smem] + [hbm] * 6, ring(F, TILE) + ring(D, TILE // 4), 6 * block)(place, wg, wu, wd, *side)
@@ -269,12 +269,15 @@
         w2 = later(both_kernel, lambda o, j: rows_of(o, j, 0), got_d[0], w2, D, TILE // 4)
         w2 = later(first_kernel, lambda o, j: rows_of(o, j, BOTH_ROWS), got_d[1], w2, D, TILE // 2,
                    vmem)
-        r = BOTH_ROWS
-        for got in got_d[2:]:
-            w2 = call(functools.partial(last_kernel, lambda o, j, r=r: rows_of(o, j, r)),
+        for i, got in enumerate(got_d[2:]):
+            r0, r1, c0, c1, _ = LAST[i]
+
+            def rect(out, j, r0=r0, r1=r1, c0=c0, c1=c1):
+                return out.at[j, pl.ds(r0, r1 - r0), pl.ds(c0, c1 - c0)]
+
+            w2 = call(functools.partial(last_kernel, rect),
                       shape(*w2.shape), [vmem, vmem, hbm], [pltpu.SemaphoreType.DMA((slots,))],
                       3 * got.size * 2, {2: 0})(place, got, w2)
-            r += got.shape[0]
         return w13[None], w2[None]
 
     spec_in = P(None, "ep", None, None)

time: 1010 us -> 1020 us (level)
  starting transfers between devices: 57.9 us -> 71.3 us
    ppermute x14 -> x15, starting transfers between devices: 57.9 us -> 71.3 us  [permute(): return lax.ppermute(x, axes, pairs)]
    ppermute x14 -> x15, waiting for transfers between devices: 783 us -> 780 us  [permute(): return lax.ppermute(x, axes, pairs)]
  transfers between devices with their start and end apart: 14 -> 15, of which waited for: 4 -> 5; matrix products, arithmetic and copies ran while one was open for 0% -> 0% of each run, Pallas kernels for 13% -> 14%
where the time goes in v3:
time: 1020 us
  waiting for transfers between devices  780 us (76%)
  Pallas kernels  156 us (15%)
  starting transfers between devices  71.3 us (7%)
  local copies, waits for them, and re-layouts  10.5 us (1%)
    ppermute x15, waiting for transfers between devices, permute(): return lax.ppermute(x, axes, pairs)  780 us
    pallas_call x1, Pallas kernels, hand_over(): call(own_kernel, (shape(slots, D, 2 * F), shape(slots, F, D)), [smem] + [...  73.6 us
    ppermute x15, starting transfers between devices, permute(): return lax.ppermute(x, axes, pairs)  71.3 us
    pallas_call x4, Pallas kernels, later(): call(functools.partial(kernel, dest), shape(*out.shape), [smem, hbm, rel_...  55.7 us
    pallas_call x1, Pallas kernels, hand_over(): call(cut_kernel, [shape(n_exp, BOTH_ROWS, D), shape(F - BOTH_ROWS, D)] +...  21.7 us
  transfers between devices with their start and end apart: 15, of which 5 were waited for; matrix products, arithmetic and copies ran while one was open for 0% of the time, Pallas kernels for 14%

profile of v3, /device:TPU:1, one launch (start us, length us, event | category | flops | bytes accessed | tf_op | source)
XLA Modules:
  0.0 1019.2 jit_solution(2333042933634058041)
XLA Ops:
  0.6 3.9 collective-permute-start.2
  7.2 21.7 %shard_map.62 = (bf16[2,768,4096]{2,1,0:T(8,128)(2,1)}, bf16[768,4096]{1,0:T(8,128)(2,1)S(1)}, bf16[32,512]{1,0:T(8,128)(2,1)S(1)}, bf16[656,4096]{1,0:T(8,128)(...) custom-call(s32[1,32]{1,0:T(1,128)S(1)} %copy-done.4, bf16[2,1536,4096]{2,1,0:T(8,128)(2,1)} %bitcast.6), custom_call_target="tpu_custom_call" | custom-call | bytes 50331648 | tf_op jit(solution)/shard_map/pallas_call | solution.py:254
  28.9 3.4 collective-permute-start.13
  34.2 3.4 collective-permute-start.10
  37.6 710.4 %collective-permute-done.10.got = bf16[32,512]{1,0:T(8,128)(2,1)S(1)} collective-permute-done((bf16[32,512]{1,0:T(8,128)(2,1)S(1)}, bf16[32,512]{1,0:T(8,128)(2,1)S(1)}, u32[]{:S(2)}, u32[]{:S(2)}) %collective-permute-start.10) | collective-permute-done | bytes 32800 | tf_op jit(solution)/shard_map/ppermute | solution.py:246
  749.3 11.7 %collective-permute-start.12 = (bf16[768,4096]{1,0:T(8,128)(2,1)S(1)}, bf16[768,4096]{1,0:T(8,128)(2,1)S(1)}, u32[]{:S(2)}, u32[]{:S(2)}) collective-permute-start(bf16[768,4096]{1,0:T(8,128)(2,1)S(1)} %collective-permute-done.11.got), channel_id=1, source_target_pairs={{1,0},{3,2}} | collective-permute-start | bytes 18874376 | tf_op jit(solution)/shard_map/ppermute | solution.py:246
  761.0 2.6 copy-done
  764.9 5.4 collective-permute-done.12.rel
  770.4 2.6 copy-done.2
  774.3 19.6 %collective-permute-start.3 = (bf16[2,4096,1536]{2,1,0:T(8,128)(2,1)}, bf16[2,4096,1536]{2,1,0:T(8,128)(2,1)}, u32[]{:S(2)}, u32[]{:S(2)}) collective-permute-start(bf16[2,4096,1536]{2,1,0:T(8,128)(2,1)} %collective-permute-done.2.got), channel_id=1, source_target_pairs={{1,0},{3,2}} | collective-permute-start | bytes 75497480 | tf_op jit(solution)/shard_map/ppermute | solution.py:246
  793.8 9.5 collective-permute-start.1
  805.5 17.7 %collective-permute-done.5.cu = bf16[2,4096,1536]{2,1,0:T(8,128)(2,1)S(1)} collective-permute-done((bf16[2,4096,1536]{2,1,0:T(8,128)(2,1)}, bf16[2,4096,1536]{2,1,0:T(8,128)(2,1)S(1)}, u32[]{:S(2)}, u32[]{:S(2)}) %collective-permute-start.5) | collective-permute-done | bytes 25165856 | tf_op jit(solution)/shard_map/ppermute | solution.py:246
  823.2 3.4 collective-permute-start.9
  826.6 32.8 %collective-permute-done.6.cd = bf16[2,1536,4096]{2,1,0:T(8,128)(2,1)} collective-permute-done((bf16[2,1536,4096]{2,1,0:T(8,128)(2,1)}, bf16[2,1536,4096]{2,1,0:T(8,128)(2,1)}, u32[]{:S(2)}, u32[]{:S(2)}) %collective-permute-start.6) | collective-permute-done | bytes 25165856 | tf_op jit(solution)/shard_map/ppermute | solution.py:246
  859.3 3.4 collective-permute-start.8
  862.7 13.8 %collective-permute-done.14.rel = bf16[2,768,4096]{2,1,0:T(8,128)(2,1)S(1)} collective-permute-done((bf16[2,768,4096]{2,1,0:T(8,128)(2,1)S(1)}, bf16[2,768,4096]{2,1,0:T(8,128)(2,1)S(1)}, u32[]{:S(2)}, u32[]{:S(2)}) %collective-permute-start.14) | collective-permute-done | bytes 12582944 | tf_op jit(solution)/shard_map/ppermute | solution.py:246
  876.5 4.6 copy-done.7
  881.1 3.4 collective-permute-start.7
  884.4 73.6 %shard_map.59 = (bf16[4,4096,3072]{2,1,0:T(8,128)(2,1)}, bf16[4,1536,4096]{2,1,0:T(8,128)(2,1)}) custom-call(s32[1,32]{1,0:T(1,128)S(1)} %copy-done.4, bf16[2,4096,1536]{2,1,0:T(8,128)(2,1)} %bitcast.14, bf16[2,4096,1536]{2,1,0:T(8,128)(2,1)} %bitcast.11, bf16[2,1536,4096]{2,1,0:T(8,128)(2,1)} %bitcast.8, bf16[2,4096,1536]{2,1,0:T(8,128)(2,1)} %collective-permute-done.4.cg, ...), custom_call_target="tpu_custom_call" | custom-call | bytes 150994944 | tf_op jit(solution)/shard_map/pallas_call | solution.py:259
  958.1 10.7 %shard_map.63._ = bf16[4,1536,4096]{2,1,0:T(8,128)(2,1)} custom-call(s32[1,32]{1,0:T(1,128)S(1)} %copy-done.4, bf16[2,768,4096]{2,1,0:T(8,128)(2,1)S(1)} %collective-permute-done.13.got, bf16[2,768,4096]{2,1,0:T(8,128)(2,1)} %copy-done.7, bf16[4,1536,4096]{2,1,0:T(8,128)(2,1)} %get-tuple-element.17._), custom_call_target="tpu_custom_call", output_to_operand_aliasing={{}: (3, {})} | custom-call | bytes 37748736 | tf_op jit(solution)/shard_map/pallas_call | solution.py:264
  968.8 8.5 shard_map.64._
  977.5 2.7 shard_map.66._
  982.6 18.3 %shard_map.60._ = bf16[4,4096,3072]{2,1,0:T(8,128)(2,1)} custom-call(s32[1,32]{1,0:T(1,128)S(1)} %copy-done.5, bf16[2,4096,1536]{2,1,0:T(8,128)(2,1)} %collective-permute-done.2.got, bf16[2,4096,1536]{2,1,0:T(8,128)(2,1)} %collective-permute-done.3.rel, bf16[4,4096,3072]{2,1,0:T(8,128)(2,1)} %get-tuple-element.10._), custom_call_target="tpu_custom_call", output_to_operand_aliasing={{}: (3, {})} | custom-call | bytes 75497472 | tf_op jit(solution)/shard_map/pallas_call | solution.py:264
  1001.0 18.3 %shard_map.61 = bf16[4,4096,3072]{2,1,0:T(8,128)(2,1)} custom-call(s32[1,32]{1,0:T(1,128)S(1)} %copy-done.5, bf16[2,4096,1536]{2,1,0:T(8,128)(2,1)} %collective-permute-done.got, bf16[2,4096,1536]{2,1,0:T(8,128)(2,1)} %collective-permute-done.1.rel, bf16[4,4096,3072]{2,1,0:T(8,128)(2,1)} %shard_map.60._), custom_call_target="tpu_custom_call", output_to_operand_aliasing={{}: (3, {})} | custom-call | bytes 75497472 | tf_op jit(solution)/shard_map/pallas_call | solution.py:264
  (32 shorter events, 13.1 us)
Async XLA Ops:
  0.6 773.6 %collective-permute-start.2 = (bf16[2,4096,1536]{2,1,0:T(8,128)(2,1)}, bf16[2,4096,1536]{2,1,0:T(8,128)(2,1)}, u32[]{:S(2)}, u32[]{:S(2)}) collective-permute-start(bf16[2,4096,1536]{2,1,0:T(8,128)(2,1)} %bitcast.12), channel_id=1, source_target_pairs={{3,1},{1,3},{6,4},{4,6}} | collective-permute-start | bytes 75497480 | tf_op jit(solution)/shard_map/ppermute | solution.py:246
  4.6 789.3 %collective-permute-start = (bf16[2,4096,1536]{2,1,0:T(8,128)(2,1)}, bf16[2,4096,1536]{2,1,0:T(8,128)(2,1)}, u32[]{:S(2)}, u32[]{:S(2)}) collective-permute-start(bf16[2,4096,1536]{2,1,0:T(8,128)(2,1)} %bitcast.9), channel_id=1, source_target_pairs={{3,1},{1,3},{6,4},{4,6}} | collective-permute-start | bytes 75497480 | tf_op jit(solution)/shard_map/ppermute | solution.py:246
  6.5 0.7 copy-start.4
  28.9 734.8 %collective-permute-start.13 = (bf16[2,768,4096]{2,1,0:T(8,128)(2,1)}, bf16[2,768,4096]{2,1,0:T(8,128)(2,1)S(1)}, u32[]{:S(2)}, u32[]{:S(2)}) collective-permute-start(bf16[2,768,4096]{2,1,0:T(8,128)(2,1)} %get-tuple-element.16), channel_id=1, source_target_pairs={{3,1},{1,3},{6,4},{4,6}} | collective-permute-start | bytes 37748744 | tf_op jit(solution)/shard_map/ppermute | solution.py:246
  32.3 717.0 %collective-permute-start.11 = (bf16[768,4096]{1,0:T(8,128)(2,1)S(1)}, bf16[768,4096]{1,0:T(8,128)(2,1)S(1)}, u32[]{:S(2)}, u32[]{:S(2)}) collective-permute-start(bf16[768,4096]{1,0:T(8,128)(2,1)S(1)} %get-tuple-element.15), channel_id=1, source_target_pairs={{3,1},{1,3},{6,4},{4,6}} | collective-permute-start | bytes 18874376 | tf_op jit(solution)/shard_map/ppermute | solution.py:246
  34.2 713.8 %collective-permute-start.10 = (bf16[32,512]{1,0:T(8,128)(2,1)S(1)}, bf16[32,512]{1,0:T(8,128)(2,1)S(1)}, u32[]{:S(2)}, u32[]{:S(2)}) collective-permute-start(bf16[32,512]{1,0:T(8,128)(2,1)S(1)} %get-tuple-element.14), channel_id=1, source_target_pairs={{3,1},{1,3},{2,4},{0,6}} | collective-permute-start | bytes 98312 | tf_op jit(solution)/shard_map/ppermute | solution.py:246
  748.0 55.4 %collective-permute-start.4 = (bf16[2,4096,1536]{2,1,0:T(8,128)(2,1)}, bf16[2,4096,1536]{2,1,0:T(8,128)(2,1)}, u32[]{:S(2)}, u32[]{:S(2)}) collective-permute-start(bf16[2,4096,1536]{2,1,0:T(8,128)(2,1)} %bitcast.13), channel_id=1, source_target_pairs={{0,1},{2,3}} | collective-permute-start | bytes 75497480 | tf_op jit(solution)/shard_map/ppermute | solution.py:246
  749.3 21.1 %collective-permute-start.12 = (bf16[768,4096]{1,0:T(8,128)(2,1)S(1)}, bf16[768,4096]{1,0:T(8,128)(2,1)S(1)}, u32[]{:S(2)}, u32[]{:S(2)}) collective-permute-start(bf16[768,4096]{1,0:T(8,128)(2,1)S(1)} %collective-permute-done.11.got), channel_id=1, source_target_pairs={{1,0},{3,2}} | collective-permute-start | bytes 18874376 | tf_op jit(solution)/shard_map/ppermute | solution.py:246
  761.0 2.6 copy-start
  763.6 59.6 %collective-permute-start.5 = (bf16[2,4096,1536]{2,1,0:T(8,128)(2,1)}, bf16[2,4096,1536]{2,1,0:T(8,128)(2,1)S(1)}, u32[]{:S(2)}, u32[]{:S(2)}) collective-permute-start(bf16[2,4096,1536]{2,1,0:T(8,128)(2,1)} %bitcast.10), channel_id=1, source_target_pairs={{0,1},{2,3}} | collective-permute-start | bytes 75497480 | tf_op jit(solution)/shard_map/ppermute | solution.py:246
  770.4 2.6 copy-start.2
  773.0 86.4 %collective-permute-start.6 = (bf16[2,1536,4096]{2,1,0:T(8,128)(2,1)}, bf16[2,1536,4096]{2,1,0:T(8,128)(2,1)}, u32[]{:S(2)}, u32[]{:S(2)}) collective-permute-start(bf16[2,1536,4096]{2,1,0:T(8,128)(2,1)} %bitcast.7), channel_id=1, source_target_pairs={{0,1},{2,3}} | collective-permute-start | bytes 75497480 | tf_op jit(solution)/shard_map/ppermute | solution.py:246
  774.3 208.4 %collective-permute-start.3 = (bf16[2,4096,1536]{2,1,0:T(8,128)(2,1)}, bf16[2,4096,1536]{2,1,0:T(8,128)(2,1)}, u32[]{:S(2)}, u32[]{:S(2)}) collective-permute-start(bf16[2,4096,1536]{2,1,0:T(8,128)(2,1)} %collective-permute-done.2.got), channel_id=1, source_target_pairs={{1,0},{3,2}} | collective-permute-start | bytes 75497480 | tf_op jit(solution)/shard_map/ppermute | solution.py:246
  793.8 207.1 %collective-permute-start.1 = (bf16[2,4096,1536]{2,1,0:T(8,128)(2,1)}, bf16[2,4096,1536]{2,1,0:T(8,128)(2,1)}, u32[]{:S(2)}, u32[]{:S(2)}) collective-permute-start(bf16[2,4096,1536]{2,1,0:T(8,128)(2,1)} %collective-permute-done.got), channel_id=1, source_target_pairs={{1,0},{3,2}} | collective-permute-start | bytes 75497480 | tf_op jit(solution)/shard_map/ppermute | solution.py:246
  803.4 73.1 %collective-permute-start.14 = (bf16[2,768,4096]{2,1,0:T(8,128)(2,1)S(1)}, bf16[2,768,4096]{2,1,0:T(8,128)(2,1)S(1)}, u32[]{:S(2)}, u32[]{:S(2)}) collective-permute-start(bf16[2,768,4096]{2,1,0:T(8,128)(2,1)S(1)} %collective-permute-done.13.got), channel_id=1, source_target_pairs={{1,0},{3,2}} | collective-permute-start | bytes 37748744 | tf_op jit(solution)/shard_map/ppermute | solution.py:246
  823.2 53.3 %copy-start.6 = (bf16[2,4096,1536]{2,1,0:T(8,128)(2,1)}, bf16[2,4096,1536]{2,1,0:T(8,128)(2,1)S(1)}, u32[]{:S(2)}) copy-start(bf16[2,4096,1536]{2,1,0:T(8,128)(2,1)S(1)} %collective-permute-done.5.cu) | copy-start | bytes 75497472
  823.2 154.2 %collective-permute-start.9 = (bf16[656,4096]{1,0:T(8,128)(2,1)}, bf16[656,4096]{1,0:T(8,128)(2,1)}, u32[]{:S(2)}, u32[]{:S(2)}) collective-permute-start(bf16[656,4096]{1,0:T(8,128)(2,1)} %get-tuple-element.13), channel_id=1, source_target_pairs={{3,1},{1,3},{6,4},{4,6}} | collective-permute-start | bytes 16121864 | tf_op jit(solution)/shard_map/ppermute | solution.py:246
  859.3 120.8 %collective-permute-start.8 = (bf16[80,4096]{1,0:T(8,128)(2,1)}, bf16[80,4096]{1,0:T(8,128)(2,1)}, u32[]{:S(2)}, u32[]{:S(2)}) collective-permute-start(bf16[80,4096]{1,0:T(8,128)(2,1)} %get-tuple-element.12), channel_id=1, source_target_pairs={{3,1},{1,3},{6,4},{4,6}} | collective-permute-start | bytes 1966088 | tf_op jit(solution)/shard_map/ppermute | solution.py:246
  876.5 4.6 copy-start.7
  881.1 100.4 %collective-permute-start.7 = (bf16[32,3584]{1,0:T(8,128)(2,1)}, bf16[32,3584]{1,0:T(8,128)(2,1)}, u32[]{:S(2)}, u32[]{:S(2)}) collective-permute-start(bf16[32,3584]{1,0:T(8,128)(2,1)} %get-tuple-element.11), channel_id=1, source_target_pairs={{3,1},{1,3},{6,4},{4,6}} | collective-permute-start | bytes 688136 | tf_op jit(solution)/shard_map/ppermute | solution.py:246
  958.0 10.7 %copy-start.1 = (bf16[768,4096]{1,0:T(8,128)(2,1)S(1)}, bf16[768,4096]{1,0:T(8,128)(2,1)}, u32[]{:S(2)}) copy-start(bf16[768,4096]{1,0:T(8,128)(2,1)} %copy-done) | copy-start | bytes 18874372
  958.1 10.7 %copy-start.3 = (bf16[768,4096]{1,0:T(8,128)(2,1)S(1)}, bf16[768,4096]{1,0:T(8,128)(2,1)}, u32[]{:S(2)}) copy-start(bf16[768,4096]{1,0:T(8,128)(2,1)} %copy-done.2) | copy-start | bytes 18874372
  981.5 1.2 copy-start.5

commit v4 on v3

--- a/solution.py
+++ b/solution.py
@@ -13,7 +13,7 @@
 VMEM_LIMIT = 36 * 1024 * 1024
 VMEM_LIMIT_WIDE = 44 * 1024 * 1024
 BOTH_ROWS = 768
-LAST = ((1504, 1536, 0, 512, True), (768, 1424, 0, 4096, False), (1424, 1504, 0, 4096, False), (1504, 1536, 512, 4096, False))
+LAST = ((1504, 1536, 0, 384, True), (768, 1424, 0, 4096, False), (1424, 1504, 0, 4096, False), (1504, 1536, 384, 4096, False))
 
 
 def _shard(dp, ep, slots, a, g, j):
@@ -91,6 +91,22 @@
                 pl.when(wanted[j])(go)
 
     _stream(len(tiles), read, writes)
+
+
+def _flow(blocks, buf, rsem, wsem):
+    steps = [(src.at[pl.ds(r, n)], dest(r, n), n) for src, dest in blocks
+             for r, n in _tiles(src.shape[0], buf.shape[2])]
+
+    def part(t):
+        return buf.at[t % NBUF, 0, pl.ds(0, steps[t][2])]
+
+    def read(t):
+        return pltpu.make_async_copy(steps[t][0], part(t), rsem.at[t % NBUF])
+
+    def writes(t, act):
+        act(pltpu.make_async_copy(part(t), steps[t][1], wsem.at[t % NBUF, 0]))
+
+    _stream(len(steps), read, writes)
 
 
 def solution(mesh):
@@ -167,15 +183,18 @@
                 _both(u, [half(o13, j, 1) for j in range(slots)], e, own, me, buf_f, rf, wf)
                 _both(d, [rows_of(o2, j, 0) for j in range(slots)], e, own, me, buf_d, rd, wd_)
 
+            groups = {}
             for who, blocks in ((own, (g, u, d)), (beside, (cg, cu, cd))):
                 for j in range(slots):
-                    single = [n for n in who[j] if who is beside or n not in many]
+                    single = tuple(n for n in who[j] if who is beside or n not in many)
                     if single:
-                        @pl.when(_any(me, single))
-                        def _():
-                            _one(blocks[0].at[e[j]], [half(o13, j, 0)], [True], buf_f, rf, wf)
-                            _one(blocks[1].at[e[j]], [half(o13, j, 1)], [True], buf_f, rf, wf)
-                            _one(blocks[2].at[e[j]], [rows_of(o2, j, 0)], [True], buf_d, rd, wd_)
+                        groups.setdefault(single, []).append((blocks, j))
+            for single, items in groups.items():
+                @pl.when(_any(me, single))
+                def _():
+                    _flow([(blocks[k].at[e[j]], half(o13, j, k)) for blocks, j in items for k in range(2)],
+                          buf_f, rf, wf)
+                    _flow([(blocks[2].at[e[j]], rows_of(o2, j, 0)) for blocks, j in items], buf_d, rd, wd_)
 
         def both_kernel(dest, place_ref, got, rel, _, out, buf, rs, ws):
             me = where()

time: 1020 us -> 1020 us (level)
  transfers between devices with their start and end apart: 15 -> 15, of which waited for: 5 -> 5; matrix products, arithmetic and copies ran while one was open for 0% -> 0% of each run, Pallas kernels for 14% -> 13%
where the time goes in v4:
time: 1020 us
  waiting for transfers between devices  780 us (76%)
  Pallas kernels  153 us (15%)
  starting transfers between devices  71.3 us (7%)
  local copies, waits for them, and re-layouts  10.5 us (1%)
    ppermute x15, waiting for transfers between devices, permute(): return lax.ppermute(x, axes, pairs)  780 us
    ppermute x15, starting transfers between devices, permute(): return lax.ppermute(x, axes, pairs)  71.3 us
    pallas_call x1, Pallas kernels, hand_over(): call(own_kernel, (shape(slots, D, 2 * F), shape(slots, F, D)), [smem] + [...  70 us
    pallas_call x4, Pallas kernels, later(): call(functools.partial(kernel, dest), shape(*out.shape), [smem, hbm, rel_...  55.7 us
    pallas_call x1, Pallas kernels, hand_over(): call(cut_kernel, [shape(n_exp, BOTH_ROWS, D), shape(F - BOTH_ROWS, D)] +...  21.7 us
  transfers between devices with their start and end apart: 15, of which 5 were waited for; matrix products, arithmetic and copies ran while one was open for 0% of the time, Pallas kernels for 13%

profile of v4, /device:TPU:1, one launch (start us, length us, event | category | flops | bytes accessed | tf_op | source)
XLA Modules:
  0.0 1015.4 jit_solution(5179833131733930268)
XLA Ops:
  0.6 3.9 collective-permute-start.2
  7.2 21.7 %shard_map.62 = (bf16[2,768,4096]{2,1,0:T(8,128)(2,1)}, bf16[768,4096]{1,0:T(8,128)(2,1)S(1)}, bf16[32,384]{1,0:T(8,128)(2,1)S(1)}, bf16[656,4096]{1,0:T(8,128)(...) custom-call(s32[1,32]{1,0:T(1,128)S(1)} %copy-done.4, bf16[2,1536,4096]{2,1,0:T(8,128)(2,1)} %bitcast.6), custom_call_target="tpu_custom_call" | custom-call | bytes 50331648 | tf_op jit(solution)/shard_map/pallas_call | solution.py:273
  28.9 3.4 collective-permute-start.13
  34.2 3.4 collective-permute-start.10
  37.6 710.2 %collective-permute-done.10.got = bf16[32,384]{1,0:T(8,128)(2,1)S(1)} collective-permute-done((bf16[32,384]{1,0:T(8,128)(2,1)S(1)}, bf16[32,384]{1,0:T(8,128)(2,1)S(1)}, u32[]{:S(2)}, u32[]{:S(2)}) %collective-permute-start.10) | collective-permute-done | bytes 24608 | tf_op jit(solution)/shard_map/ppermute | solution.py:265
  749.1 11.7 %collective-permute-start.12 = (bf16[768,4096]{1,0:T(8,128)(2,1)S(1)}, bf16[768,4096]{1,0:T(8,128)(2,1)S(1)}, u32[]{:S(2)}, u32[]{:S(2)}) collective-permute-start(bf16[768,4096]{1,0:T(8,128)(2,1)S(1)} %collective-permute-done.11.got), channel_id=1, source_target_pairs={{1,0},{3,2}} | collective-permute-start | bytes 18874376 | tf_op jit(solution)/shard_map/ppermute | solution.py:265
  760.8 2.6 copy-done
  764.8 5.4 collective-permute-done.12.rel
  770.2 2.6 copy-done.2
  774.1 19.6 %collective-permute-start.3 = (bf16[2,4096,1536]{2,1,0:T(8,128)(2,1)}, bf16[2,4096,1536]{2,1,0:T(8,128)(2,1)}, u32[]{:S(2)}, u32[]{:S(2)}) collective-permute-start(bf16[2,4096,1536]{2,1,0:T(8,128)(2,1)} %collective-permute-done.2.got), channel_id=1, source_target_pairs={{1,0},{3,2}} | collective-permute-start | bytes 75497480 | tf_op jit(solution)/shard_map/ppermute | solution.py:265
  793.7 9.5 collective-permute-start.1
  805.3 17.7 %collective-permute-done.5.cu = bf16[2,4096,1536]{2,1,0:T(8,128)(2,1)S(1)} collective-permute-done((bf16[2,4096,1536]{2,1,0:T(8,128)(2,1)}, bf16[2,4096,1536]{2,1,0:T(8,128)(2,1)S(1)}, u32[]{:S(2)}, u32[]{:S(2)}) %collective-permute-start.5) | collective-permute-done | bytes 25165856 | tf_op jit(solution)/shard_map/ppermute | solution.py:265
  823.0 3.4 collective-permute-start.9
  826.4 32.8 %collective-permute-done.6.cd = bf16[2,1536,4096]{2,1,0:T(8,128)(2,1)} collective-permute-done((bf16[2,1536,4096]{2,1,0:T(8,128)(2,1)}, bf16[2,1536,4096]{2,1,0:T(8,128)(2,1)}, u32[]{:S(2)}, u32[]{:S(2)}) %collective-permute-start.6) | collective-permute-done | bytes 25165856 | tf_op jit(solution)/shard_map/ppermute | solution.py:265
  859.2 3.4 collective-permute-start.8
  862.5 13.8 %collective-permute-done.14.rel = bf16[2,768,4096]{2,1,0:T(8,128)(2,1)S(1)} collective-permute-done((bf16[2,768,4096]{2,1,0:T(8,128)(2,1)S(1)}, bf16[2,768,4096]{2,1,0:T(8,128)(2,1)S(1)}, u32[]{:S(2)}, u32[]{:S(2)}) %collective-permute-start.14) | collective-permute-done | bytes 12582944 | tf_op jit(solution)/shard_map/ppermute | solution.py:265
  876.3 4.6 copy-done.7
  880.9 3.4 collective-permute-start.7
  884.2 70.0 %shard_map.59 = (bf16[4,4096,3072]{2,1,0:T(8,128)(2,1)}, bf16[4,1536,4096]{2,1,0:T(8,128)(2,1)}) custom-call(s32[1,32]{1,0:T(1,128)S(1)} %copy-done.4, bf16[2,4096,1536]{2,1,0:T(8,128)(2,1)} %bitcast.14, bf16[2,4096,1536]{2,1,0:T(8,128)(2,1)} %bitcast.11, bf16[2,1536,4096]{2,1,0:T(8,128)(2,1)} %bitcast.8, bf16[2,4096,1536]{2,1,0:T(8,128)(2,1)} %collective-permute-done.4.cg, ...), custom_call_target="tpu_custom_call" | custom-call | bytes 150994944 | tf_op jit(solution)/shard_map/pallas_call | solution.py:278
  954.2 10.7 %shard_map.63._ = bf16[4,1536,4096]{2,1,0:T(8,128)(2,1)} custom-call(s32[1,32]{1,0:T(1,128)S(1)} %copy-done.4, bf16[2,768,4096]{2,1,0:T(8,128)(2,1)S(1)} %collective-permute-done.13.got, bf16[2,768,4096]{2,1,0:T(8,128)(2,1)} %copy-done.7, bf16[4,1536,4096]{2,1,0:T(8,128)(2,1)} %get-tuple-element.17._), custom_call_target="tpu_custom_call", output_to_operand_aliasing={{}: (3, {})} | custom-call | bytes 37748736 | tf_op jit(solution)/shard_map/pallas_call | solution.py:283
  965.0 8.5 shard_map.64._
  973.6 2.7 shard_map.66._
  978.8 18.3 %shard_map.60._ = bf16[4,4096,3072]{2,1,0:T(8,128)(2,1)} custom-call(s32[1,32]{1,0:T(1,128)S(1)} %copy-done.5, bf16[2,4096,1536]{2,1,0:T(8,128)(2,1)} %collective-permute-done.2.got, bf16[2,4096,1536]{2,1,0:T(8,128)(2,1)} %collective-permute-done.3.rel, bf16[4,4096,3072]{2,1,0:T(8,128)(2,1)} %get-tuple-element.10._), custom_call_target="tpu_custom_call", output_to_operand_aliasing={{}: (3, {})} | custom-call | bytes 75497472 | tf_op jit(solution)/shard_map/pallas_call | solution.py:283
  997.1 18.3 %shard_map.61 = bf16[4,4096,3072]{2,1,0:T(8,128)(2,1)} custom-call(s32[1,32]{1,0:T(1,128)S(1)} %copy-done.5, bf16[2,4096,1536]{2,1,0:T(8,128)(2,1)} %collective-permute-done.got, bf16[2,4096,1536]{2,1,0:T(8,128)(2,1)} %collective-permute-done.1.rel, bf16[4,4096,3072]{2,1,0:T(8,128)(2,1)} %shard_map.60._), custom_call_target="tpu_custom_call", output_to_operand_aliasing={{}: (3, {})} | custom-call | bytes 75497472 | tf_op jit(solution)/shard_map/pallas_call | solution.py:283
  (32 shorter events, 13.1 us)
Async XLA Ops:
  0.6 773.5 %collective-permute-start.2 = (bf16[2,4096,1536]{2,1,0:T(8,128)(2,1)}, bf16[2,4096,1536]{2,1,0:T(8,128)(2,1)}, u32[]{:S(2)}, u32[]{:S(2)}) collective-permute-start(bf16[2,4096,1536]{2,1,0:T(8,128)(2,1)} %bitcast.12), channel_id=1, source_target_pairs={{3,1},{1,3},{6,4},{4,6}} | collective-permute-start | bytes 75497480 | tf_op jit(solution)/shard_map/ppermute | solution.py:265
  4.6 789.1 %collective-permute-start = (bf16[2,4096,1536]{2,1,0:T(8,128)(2,1)}, bf16[2,4096,1536]{2,1,0:T(8,128)(2,1)}, u32[]{:S(2)}, u32[]{:S(2)}) collective-permute-start(bf16[2,4096,1536]{2,1,0:T(8,128)(2,1)} %bitcast.9), channel_id=1, source_target_pairs={{3,1},{1,3},{6,4},{4,6}} | collective-permute-start | bytes 75497480 | tf_op jit(solution)/shard_map/ppermute | solution.py:265
  6.5 0.7 copy-start.4
  28.9 734.6 %collective-permute-start.13 = (bf16[2,768,4096]{2,1,0:T(8,128)(2,1)}, bf16[2,768,4096]{2,1,0:T(8,128)(2,1)S(1)}, u32[]{:S(2)}, u32[]{:S(2)}) collective-permute-start(bf16[2,768,4096]{2,1,0:T(8,128)(2,1)} %get-tuple-element.16), channel_id=1, source_target_pairs={{3,1},{1,3},{6,4},{4,6}} | collective-permute-start | bytes 37748744 | tf_op jit(solution)/shard_map/ppermute | solution.py:265
  32.3 716.8 %collective-permute-start.11 = (bf16[768,4096]{1,0:T(8,128)(2,1)S(1)}, bf16[768,4096]{1,0:T(8,128)(2,1)S(1)}, u32[]{:S(2)}, u32[]{:S(2)}) collective-permute-start(bf16[768,4096]{1,0:T(8,128)(2,1)S(1)} %get-tuple-element.15), channel_id=1, source_target_pairs={{3,1},{1,3},{6,4},{4,6}} | collective-permute-start | bytes 18874376 | tf_op jit(solution)/shard_map/ppermute | solution.py:265
  34.2 713.6 %collective-permute-start.10 = (bf16[32,384]{1,0:T(8,128)(2,1)S(1)}, bf16[32,384]{1,0:T(8,128)(2,1)S(1)}, u32[]{:S(2)}, u32[]{:S(2)}) collective-permute-start(bf16[32,384]{1,0:T(8,128)(2,1)S(1)} %get-tuple-element.14), channel_id=1, source_target_pairs={{3,1},{1,3},{2,4},{0,6}} | collective-permute-start | bytes 73736 | tf_op jit(solution)/shard_map/ppermute | solution.py:265
  747.8 55.4 %collective-permute-start.4 = (bf16[2,4096,1536]{2,1,0:T(8,128)(2,1)}, bf16[2,4096,1536]{2,1,0:T(8,128)(2,1)}, u32[]{:S(2)}, u32[]{:S(2)}) collective-permute-start(bf16[2,4096,1536]{2,1,0:T(8,128)(2,1)} %bitcast.13), channel_id=1, source_target_pairs={{0,1},{2,3}} | collective-permute-start | bytes 75497480 | tf_op jit(solution)/shard_map/ppermute | solution.py:265
  749.1 21.1 %collective-permute-start.12 = (bf16[768,4096]{1,0:T(8,128)(2,1)S(1)}, bf16[768,4096]{1,0:T(8,128)(2,1)S(1)}, u32[]{:S(2)}, u32[]{:S(2)}) collective-permute-start(bf16[768,4096]{1,0:T(8,128)(2,1)S(1)} %collective-permute-done.11.got), channel_id=1, source_target_pairs={{1,0},{3,2}} | collective-permute-start | bytes 18874376 | tf_op jit(solution)/shard_map/ppermute | solution.py:265
  760.8 2.6 copy-start
  763.5 59.6 %collective-permute-start.5 = (bf16[2,4096,1536]{2,1,0:T(8,128)(2,1)}, bf16[2,4096,1536]{2,1,0:T(8,128)(2,1)S(1)}, u32[]{:S(2)}, u32[]{:S(2)}) collective-permute-start(bf16[2,4096,1536]{2,1,0:T(8,128)(2,1)} %bitcast.10), channel_id=1, source_target_pairs={{0,1},{2,3}} | collective-permute-start | bytes 75497480 | tf_op jit(solution)/shard_map/ppermute | solution.py:265
  770.2 2.6 copy-start.2
  772.8 86.4 %collective-permute-start.6 = (bf16[2,1536,4096]{2,1,0:T(8,128)(2,1)}, bf16[2,1536,4096]{2,1,0:T(8,128)(2,1)}, u32[]{:S(2)}, u32[]{:S(2)}) collective-permute-start(bf16[2,1536,4096]{2,1,0:T(8,128)(2,1)} %bitcast.7), channel_id=1, source_target_pairs={{0,1},{2,3}} | collective-permute-start | bytes 75497480 | tf_op jit(solution)/shard_map/ppermute | solution.py:265
  774.1 204.7 %collective-permute-start.3 = (bf16[2,4096,1536]{2,1,0:T(8,128)(2,1)}, bf16[2,4096,1536]{2,1,0:T(8,128)(2,1)}, u32[]{:S(2)}, u32[]{:S(2)}) collective-permute-start(bf16[2,4096,1536]{2,1,0:T(8,128)(2,1)} %collective-permute-done.2.got), channel_id=1, source_target_pairs={{1,0},{3,2}} | collective-permute-start | bytes 75497480 | tf_op jit(solution)/shard_map/ppermute | solution.py:265
  793.7 203.4 %collective-permute-start.1 = (bf16[2,4096,1536]{2,1,0:T(8,128)(2,1)}, bf16[2,4096,1536]{2,1,0:T(8,128)(2,1)}, u32[]{:S(2)}, u32[]{:S(2)}) collective-permute-start(bf16[2,4096,1536]{2,1,0:T(8,128)(2,1)} %collective-permute-done.got), channel_id=1, source_target_pairs={{1,0},{3,2}} | collective-permute-start | bytes 75497480 | tf_op jit(solution)/shard_map/ppermute | solution.py:265
  803.2 73.1 %collective-permute-start.14 = (bf16[2,768,4096]{2,1,0:T(8,128)(2,1)S(1)}, bf16[2,768,4096]{2,1,0:T(8,128)(2,1)S(1)}, u32[]{:S(2)}, u32[]{:S(2)}) collective-permute-start(bf16[2,768,4096]{2,1,0:T(8,128)(2,1)S(1)} %collective-permute-done.13.got), channel_id=1, source_target_pairs={{1,0},{3,2}} | collective-permute-start | bytes 37748744 | tf_op jit(solution)/shard_map/ppermute | solution.py:265
  823.0 53.3 %copy-start.6 = (bf16[2,4096,1536]{2,1,0:T(8,128)(2,1)}, bf16[2,4096,1536]{2,1,0:T(8,128)(2,1)S(1)}, u32[]{:S(2)}) copy-start(bf16[2,4096,1536]{2,1,0:T(8,128)(2,1)S(1)} %collective-permute-done.5.cu) | copy-start | bytes 75497472
  823.0 150.6 %collective-permute-start.9 = (bf16[656,4096]{1,0:T(8,128)(2,1)}, bf16[656,4096]{1,0:T(8,128)(2,1)}, u32[]{:S(2)}, u32[]{:S(2)}) collective-permute-start(bf16[656,4096]{1,0:T(8,128)(2,1)} %get-tuple-element.13), channel_id=1, source_target_pairs={{3,1},{1,3},{6,4},{4,6}} | collective-permute-start | bytes 16121864 | tf_op jit(solution)/shard_map/ppermute | solution.py:265
  859.2 117.2 %collective-permute-start.8 = (bf16[80,4096]{1,0:T(8,128)(2,1)}, bf16[80,4096]{1,0:T(8,128)(2,1)}, u32[]{:S(2)}, u32[]{:S(2)}) collective-permute-start(bf16[80,4096]{1,0:T(8,128)(2,1)} %get-tuple-element.12), channel_id=1, source_target_pairs={{3,1},{1,3},{6,4},{4,6}} | collective-permute-start | bytes 1966088 | tf_op jit(solution)/shard_map/ppermute | solution.py:265
  876.3 4.6 copy-start.7
  880.9 96.8 %collective-permute-start.7 = (bf16[32,3712]{1,0:T(8,128)(2,1)}, bf16[32,3712]{1,0:T(8,128)(2,1)}, u32[]{:S(2)}, u32[]{:S(2)}) collective-permute-start(bf16[32,3712]{1,0:T(8,128)(2,1)} %get-tuple-element.11), channel_id=1, source_target_pairs={{3,1},{1,3},{6,4},{4,6}} | collective-permute-start | bytes 712712 | tf_op jit(solution)/shard_map/ppermute | solution.py:265
  954.2 10.7 %copy-start.1 = (bf16[768,4096]{1,0:T(8,128)(2,1)S(1)}, bf16[768,4096]{1,0:T(8,128)(2,1)}, u32[]{:S(2)}) copy-start(bf16[768,4096]{1,0:T(8,128)(2,1)} %copy-done) | copy-start | bytes 18874372
  954.2 10.7 %copy-start.3 = (bf16[768,4096]{1,0:T(8,128)(2,1)S(1)}, bf16[768,4096]{1,0:T(8,128)(2,1)}, u32[]{:S(2)}) copy-start(bf16[768,4096]{1,0:T(8,128)(2,1)} %copy-done.2) | copy-start | bytes 18874372
  977.6 1.2 copy-start.5
